TPU v7x, 128 devices: a whole 4x4x4 slice. The times are simulated.
128 devices in a mesh: graph: 1, nodes: 128 (over z, y, x, core).
Axes of the slice: x: 4, y: 4, z: 4, core: 2. Of those that a mesh axis runs over, the one named last changes fastest.
Arguments:
- node_feats: bfloat16 [131072, 300], P(('graph', 'nodes'))
- a_int: bfloat16 [131072, 1024], P(('graph', 'nodes'))
- a_halo: bfloat16 [131072, 512], P(('graph', 'nodes'))
- send_idx: int32 [512, 128], P(('graph', 'nodes'))
- w_first: bfloat16 [300, 512], replicated
- w_second: bfloat16 [512, 100], replicated
- grad_out: bfloat16 [131072, 100], P(('graph', 'nodes'))
Outputs:
- output 1: float32 [300, 512], P('graph')
- output 2: float32 [512, 100], P('graph')
- output 3: float32 [131072, 300], P(('graph', 'nodes'))
All inputs are finite; a program needn't handle non-finite values.
Results may differ from a plain program's by a relative error of at most 0.00627.
Values are sent between devices in bfloat16 or wider.
A program may use at most 1 GiB of HBM per device.

v0:
```python
import jax
import jax.numpy as jnp
from jax import lax
from jax.sharding import PartitionSpec as P


def link_offsets(num_links):
    return [(link // 2 + 1) * (1 - 2 * (link % 2)) for link in range(num_links)]


def shift_pairs(axis_size, offset):
    return [(source, (source + offset) % axis_size) for source in range(axis_size)]


def contract_rows(left_rows, right_rows):
    return lax.dot_general(left_rows, right_rows, (((0,), (0,)), ((), ())), preferred_element_type=jnp.float32)


def halo_rows(features, send_idx, axis_size):
    sent_rows = jnp.take(features, send_idx, axis=0)
    received = [lax.ppermute(sent_rows[link], "nodes", shift_pairs(axis_size, offset)) for link, offset in enumerate(link_offsets(send_idx.shape[0]))]
    return jnp.concatenate(received, axis=0)


def aggregate(a_int, a_halo, features, send_idx, axis_size):
    remote = halo_rows(features, send_idx, axis_size)
    return jnp.dot(a_int, features, preferred_element_type=jnp.float32) + jnp.dot(a_halo, remote, preferred_element_type=jnp.float32)


def aggregate_back(a_int, a_halo, grad_rows, send_idx, axis_size):
    num_slots = send_idx.shape[1]
    inner_sum = contract_rows(a_int, grad_rows)
    outward = contract_rows(a_halo, grad_rows).astype(jnp.bfloat16)
    received = [lax.ppermute(outward[link * num_slots:(link + 1) * num_slots], "nodes", shift_pairs(axis_size, -offset)) for link, offset in enumerate(link_offsets(send_idx.shape[0]))]
    returned = jnp.concatenate(received, axis=0).astype(jnp.float32)
    return inner_sum.at[send_idx.reshape(-1)].add(returned)


def solution(mesh):
    axis_size = mesh.shape["nodes"]
    row_spec = P(("graph", "nodes"), None)
    replicated = P(None, None)
    part_spec = P("graph", None)

    def device_step(node_feats, a_int, a_halo, send_idx, w_first, w_second, grad_out):
        z_first = aggregate(a_int, a_halo, node_feats, send_idx, axis_size).astype(jnp.bfloat16)
        hidden = jnp.maximum(jnp.dot(z_first, w_first, preferred_element_type=jnp.float32), 0.0).astype(jnp.bfloat16)
        z_second = aggregate(a_int, a_halo, hidden, send_idx, axis_size).astype(jnp.bfloat16)
        dw_second = lax.psum(contract_rows(z_second, grad_out), "nodes")
        dz_second = lax.dot_general(grad_out, w_second, (((1,), (1,)), ((), ())), preferred_element_type=jnp.float32).astype(jnp.bfloat16)
        d_hidden = aggregate_back(a_int, a_halo, dz_second, send_idx, axis_size)
        grad_pre = jnp.where(hidden > 0, d_hidden, 0.0).astype(jnp.bfloat16)
        dw_first = lax.psum(contract_rows(z_first, grad_pre), "nodes")
        dz_first = lax.dot_general(grad_pre, w_first, (((1,), (1,)), ((), ())), preferred_element_type=jnp.float32).astype(jnp.bfloat16)
        grad_feats = aggregate_back(a_int, a_halo, dz_first, send_idx, axis_size)
        return dw_first, dw_second, grad_feats

    return jax.shard_map(device_step, mesh=mesh, in_specs=(row_spec, row_spec, row_spec, row_spec, replicated, replicated, row_spec), out_specs=(part_spec, part_spec, row_spec), check_vma=False)
```

profile of v0, /device:TPU:1, one launch (start us, length us, event | category | flops | bytes accessed | tf_op | source)
XLA Modules:
  0.0 261.3 jit_solution(16997940964678235700)
XLA Ops:
  10.2 1.9 gather_fusion
  13.1 2.6 collective-permute-start
  15.7 6.6 %collective-permute-start.3 = (bf16[128,300]{1,0:T(8,128)(2,1)}, bf16[128,300]{1,0:T(8,128)(2,1)}, u32[]{:S(2)}, u32[]{:S(2)}) collective-permute-start(bf16[128,300]{1,0:T(8,128)(2,1)} %get-tuple-element.17), channel_id=1, source_target_pairs={{0,126},{1,127},{2,0},{3,1},{4,2},{5,3},{6,4},{7,5},{8,6},{9,7},{1... | collective-permute-start | bytes 230408 | tf_op jit(solution)/shard_map/ppermute | solution.py:21
  26.2 6.3 %collective-permute-start.4 = (bf16[128,512]{0,1:T(8,128)(2,1)}, bf16[128,512]{0,1:T(8,128)(2,1)}, u32[]{:S(2)}, u32[]{:S(2)}) collective-permute-start(bf16[128,512]{0,1:T(8,128)(2,1)} %get-tuple-element.12), channel_id=1, source_target_pairs={{0,127},{1,0},{2,1},{3,2},{4,3},{5,4},{6,5},{7,6},{8,7},{9,8},{10,... | collective-permute-start | bytes 393224 | tf_op jit(solution)/shard_map/ppermute | solution.py:34
  32.5 2.6 %convolution_bitcast_fusion = f32[1024,512]{0,1:T(8,128)} fusion(bf16[1024,512]{1,0:T(8,128)(2,1)S(1)} %convolution_convert_fusion, bf16[1024,1024]{1,0:T(8,128)(2,1)S(1)} %copy-done), kind=kOutput, calls=%fused_computation.7 | convolution fusion | flops 1073741824 | bytes 5242880 | tf_op jit(solution)/shard_map/dot_general | solution.py:16
  36.6 2.9 %copy.11 = f32[1024,512]{1,0:T(8,128)} copy(f32[1024,512]{0,1:T(8,128)} %convolution_bitcast_fusion) | data formatting | bytes 4194304 | tf_op jit(solution)/shard_map/dot_general | solution.py:16
  39.5 6.9 %collective-permute-start.6 = (bf16[128,512]{0,1:T(8,128)(2,1)}, bf16[128,512]{0,1:T(8,128)(2,1)}, u32[]{:S(2)}, u32[]{:S(2)}) collective-permute-start(bf16[128,512]{0,1:T(8,128)(2,1)} %get-tuple-element.14), channel_id=1, source_target_pairs={{0,126},{1,127},{2,0},{3,1},{4,2},{5,3},{6,4},{7,5},{8,6},{9,7},{1... | collective-permute-start | bytes 393224 | tf_op jit(solution)/shard_map/ppermute | solution.py:34
  46.4 2.1 fusion.2
  50.1 2.6 %gather_fusion.1 = bf16[512,512]{1,0:T(8,128)(2,1)} fusion(bf16[1024,512]{1,0:T(8,128)(2,1)S(1)} %maximum_convert_fusion, s32[1024]{0:T(1024)S(1)} %copy-done.16), kind=kCustom, calls=%fused_computation.1 | custom fusion | bytes 1050624 | tf_op jit(solution)/shard_map/jit(_take)/gather | solution.py:20
  52.7 2.6 %fusion.34 = f32[512,1024]{1,0:T(8,128)} fusion(bf16[1024,512]{1,0:T(8,128)(2,1)S(1)} %maximum_convert_fusion, bf16[1024,1024]{1,0:T(8,128)(2,1)S(1)} %copy-done), kind=kOutput, calls=%fused_computation.56 | convolution fusion | flops 1073741824 | bytes 5242880 | tf_op jit(solution)/shard_map/dot_general | solution.py:27
  56.3 8.6 %collective-permute-start.11 = (bf16[128,512]{1,0:T(8,128)(2,1)}, bf16[128,512]{1,0:T(8,128)(2,1)}, u32[]{:S(2)}, u32[]{:S(2)}) collective-permute-start(bf16[128,512]{1,0:T(8,128)(2,1)} %get-tuple-element.9), channel_id=1, source_target_pairs={{0,126},{1,127},{2,0},{3,1},{4,2},{5,3},{6,4},{7,5},{8,6},{9,7},{1... | collective-permute-start | bytes 393224 | tf_op jit(solution)/shard_map/ppermute | solution.py:21
  65.9 2.1 maximum_convert_fusion.1
  68.0 2.6 copy.12
  70.6 7.3 %scatter_fusion = f32[1024,512]{1,0:T(8,128)} fusion(f32[1024,512]{1,0:T(8,128)} %copy.11, s32[512]{0:T(512)S(1)} %bitcast.60, f32[512,512]{1,0:T(8,128)} %copy.12), kind=kCustom, calls=%fused_computation.2 | custom fusion | flops 262144 | bytes 3147776 | tf_op jit(solution)/shard_map/scatter-add | solution.py:36
  77.9 3.3 %fusion.30 = f32[300,512]{1,0:T(8,128)} fusion(bf16[1024,300]{0,1:T(8,128)(2,1)} %copy-done.2, f32[1024,512]{1,0:T(8,128)} %scatter_fusion, bf16[1024,512]{1,0:T(8,128)(2,1)S(1)} %maximum_convert_fusion), kind=kOutput, calls=%fused_computation.52 | convolution fusion | flops 316669952 | bytes 4374528 | tf_op jit(solution)/shard_map/dot_general | solution.py:16
  84.0 6.4 %collective-permute-start.12 = (bf16[128,300]{0,1:T(8,128)(2,1)}, bf16[128,300]{0,1:T(8,128)(2,1)}, u32[]{:S(2)}, u32[]{:S(2)}) collective-permute-start(bf16[128,300]{0,1:T(8,128)(2,1)} %get-tuple-element.20), channel_id=1, source_target_pairs={{0,127},{1,0},{2,1},{3,2},{4,3},{5,4},{6,5},{7,6},{8,7},{9,8},{10,... | collective-permute-start | bytes 230408 | tf_op jit(solution)/shard_map/ppermute | solution.py:34
  90.4 6.9 %collective-permute-start.14 = (bf16[128,300]{0,1:T(8,128)(2,1)}, bf16[128,300]{0,1:T(8,128)(2,1)}, u32[]{:S(2)}, u32[]{:S(2)}) collective-permute-start(bf16[128,300]{0,1:T(8,128)(2,1)} %get-tuple-element.22), channel_id=1, source_target_pairs={{0,126},{1,127},{2,0},{3,1},{4,2},{5,3},{6,4},{7,5},{8,6},{9,7},{1... | collective-permute-start | bytes 230408 | tf_op jit(solution)/shard_map/ppermute | solution.py:34
  97.3 3.6 %fusion.1 = f32[512,100]{0,1:T(8,128)} fusion(bf16[1024,100]{0,1:T(8,128)(2,1)S(1)} %copy-done.11, f32[512,1024]{1,0:T(8,128)} %fusion.34, bf16[1024,512]{1,0:T(8,128)(2,1)S(1)} %copy-done.6, bf16[128,512]{1,0:T(8,128)(2,1)} %collective-permute-done.11, bf16[128,512]{1,0:T(8,128)(2,1)} %collective-permute-done.10, ...), kind=kOutput, calls=%fused_computation.12 | convolution fusion | flops 644874240 | bytes 4079616 | tf_op jit(solution)/shard_map/dot_general | solution.py:16
  100.9 1.9 convolution_bitcast_fusion.2
  102.8 1.6 copy.13
  105.8 6.3 %scatter_fusion.1 = f32[1024,300]{1,0:T(8,128)} fusion(f32[1024,300]{1,0:T(8,128)} %copy.13, s32[512]{0:T(512)S(1)} %bitcast.61, f32[512,300]{1,0:T(8,128)S(1)} %copy.14), kind=kCustom, calls=%fused_computation.3 | custom fusion | flops 153600 | bytes 1845248 | tf_op jit(solution)/shard_map/scatter-add | solution.py:36
  112.1 2.9 %copy.15 = f32[1024,300]{0,1:T(8,128)} copy(f32[1024,300]{1,0:T(8,128)} %scatter_fusion.1) | data formatting | bytes 2457600
  115.0 135.9 %all-reduce.3.cloned.1.call-done = (f32[300,512]{1,0:T(8,128)}, f32[512,100]{0,1:T(8,128)}) async-done(((f32[300,512]{1,0:T(8,128)}, f32[512,100]{0,1:T(8,128)}), (f32[300,512]{1,0:T(8,128)}, f32[512,100]{0,1:T(8,128)})) %all-reduce.3.cloned.1.call-update) | async-done | bytes 819216 | tf_op jit(solution)/shard_map/psum | solution.py:53
  250.8 1.9 copy.20
  (85 shorter events, 18.4 us)
Async XLA Ops:
  7.2 25.4 %copy-start = (bf16[1024,1024]{1,0:T(8,128)(2,1)S(1)}, bf16[1024,1024]{1,0:T(8,128)(2,1)}, u32[]{:S(2)}) copy-start(bf16[1024,1024]{1,0:T(8,128)(2,1)} %param.8) | copy-start | bytes 6291460
  7.2 243.7 %all-reduce.3.cloned.1.call-start = ((), (), s32[]{:S(2)}) async-start(), calls=%async_computation | async-start | bytes 1671168 | tf_op jit(solution)/shard_map/psum | solution.py:53
  10.2 13.1 %copy-start.11 = (bf16[1024,100]{0,1:T(8,128)(2,1)S(1)}, bf16[1024,100]{0,1:T(8,128)(2,1)}, u32[]{:S(2)}) copy-start(bf16[1024,100]{0,1:T(8,128)(2,1)} %param.13) | copy-start | bytes 614404
  12.2 12.5 %copy-start.4 = (bf16[1024,512]{1,0:T(8,128)(2,1)S(1)}, bf16[1024,512]{1,0:T(8,128)(2,1)}, u32[]{:S(2)}) copy-start(bf16[1024,512]{1,0:T(8,128)(2,1)} %param.9) | copy-start | bytes 3145732
  13.1 26.4 %collective-permute-start = (bf16[128,300]{1,0:T(8,128)(2,1)}, bf16[128,300]{1,0:T(8,128)(2,1)}, u32[]{:S(2)}, u32[]{:S(2)}) collective-permute-start(bf16[128,300]{1,0:T(8,128)(2,1)} %get-tuple-element.16), channel_id=1, source_target_pairs={{0,1},{1,2},{2,3},{3,4},{4,5},{5,6},{6,7},{7,8},{8,9},{9,10},{10,1... | collective-permute-start | bytes 230408 | tf_op jit(solution)/shard_map/ppermute | solution.py:21
  15.7 23.8 %collective-permute-start.3 = (bf16[128,300]{1,0:T(8,128)(2,1)}, bf16[128,300]{1,0:T(8,128)(2,1)}, u32[]{:S(2)}, u32[]{:S(2)}) collective-permute-start(bf16[128,300]{1,0:T(8,128)(2,1)} %get-tuple-element.17), channel_id=1, source_target_pairs={{0,126},{1,127},{2,0},{3,1},{4,2},{5,3},{6,4},{7,5},{8,6},{9,7},{1... | collective-permute-start | bytes 230408 | tf_op jit(solution)/shard_map/ppermute | solution.py:21
  22.3 24.1 %collective-permute-start.2 = (bf16[128,300]{1,0:T(8,128)(2,1)}, bf16[128,300]{1,0:T(8,128)(2,1)}, u32[]{:S(2)}, u32[]{:S(2)}) collective-permute-start(bf16[128,300]{1,0:T(8,128)(2,1)} %get-tuple-element.18), channel_id=1, source_target_pairs={{0,2},{1,3},{2,4},{3,5},{4,6},{5,7},{6,8},{7,9},{8,10},{9,11},{10,... | collective-permute-start | bytes 230408 | tf_op jit(solution)/shard_map/ppermute | solution.py:21
  22.3 24.1 %collective-permute-start.1 = (bf16[128,300]{1,0:T(8,128)(2,1)}, bf16[128,300]{1,0:T(8,128)(2,1)}, u32[]{:S(2)}, u32[]{:S(2)}) collective-permute-start(bf16[128,300]{1,0:T(8,128)(2,1)} %get-tuple-element.19), channel_id=1, source_target_pairs={{0,127},{1,0},{2,1},{3,2},{4,3},{5,4},{6,5},{7,6},{8,7},{9,8},{10,... | collective-permute-start | bytes 230408 | tf_op jit(solution)/shard_map/ppermute | solution.py:21
  26.2 9.0 %copy-start.7 = (bf16[1024,300]{0,1:T(8,128)(2,1)S(1)}, bf16[1024,300]{0,1:T(8,128)(2,1)}, u32[]{:S(2)}) copy-start(bf16[1024,300]{0,1:T(8,128)(2,1)} %param.7) | copy-start | bytes 1843204
  26.2 30.1 %collective-permute-start.4 = (bf16[128,512]{0,1:T(8,128)(2,1)}, bf16[128,512]{0,1:T(8,128)(2,1)}, u32[]{:S(2)}, u32[]{:S(2)}) collective-permute-start(bf16[128,512]{0,1:T(8,128)(2,1)} %get-tuple-element.12), channel_id=1, source_target_pairs={{0,127},{1,0},{2,1},{3,2},{4,3},{5,4},{6,5},{7,6},{8,7},{9,8},{10,... | collective-permute-start | bytes 393224 | tf_op jit(solution)/shard_map/ppermute | solution.py:34
  39.5 9.9 %copy-start.9 = (bf16[300,512]{1,0:T(8,128)(2,1)S(1)}, bf16[300,512]{1,0:T(8,128)(2,1)}, u32[]{:S(2)}) copy-start(bf16[300,512]{1,0:T(8,128)(2,1)} %param.11) | copy-start | bytes 921604
  39.5 25.4 %collective-permute-start.7 = (bf16[128,512]{0,1:T(8,128)(2,1)}, bf16[128,512]{0,1:T(8,128)(2,1)}, u32[]{:S(2)}, u32[]{:S(2)}) collective-permute-start(bf16[128,512]{0,1:T(8,128)(2,1)} %get-tuple-element.13), channel_id=1, source_target_pairs={{0,2},{1,3},{2,4},{3,5},{4,6},{5,7},{6,8},{7,9},{8,10},{9,11},{10,... | collective-permute-start | bytes 393224 | tf_op jit(solution)/shard_map/ppermute | solution.py:34
  39.5 25.4 %collective-permute-start.6 = (bf16[128,512]{0,1:T(8,128)(2,1)}, bf16[128,512]{0,1:T(8,128)(2,1)}, u32[]{:S(2)}, u32[]{:S(2)}) collective-permute-start(bf16[128,512]{0,1:T(8,128)(2,1)} %get-tuple-element.14), channel_id=1, source_target_pairs={{0,126},{1,127},{2,0},{3,1},{4,2},{5,3},{6,4},{7,5},{8,6},{9,7},{1... | collective-permute-start | bytes 393224 | tf_op jit(solution)/shard_map/ppermute | solution.py:34
  46.4 19.5 %collective-permute-start.5 = (bf16[128,512]{0,1:T(8,128)(2,1)}, bf16[128,512]{0,1:T(8,128)(2,1)}, u32[]{:S(2)}, u32[]{:S(2)}) collective-permute-start(bf16[128,512]{0,1:T(8,128)(2,1)} %get-tuple-element.15), channel_id=1, source_target_pairs={{0,1},{1,2},{2,3},{3,4},{4,5},{5,6},{6,7},{7,8},{8,9},{9,10},{10,1... | collective-permute-start | bytes 393224 | tf_op jit(solution)/shard_map/ppermute | solution.py:34
  56.3 14.4 %copy-start.13 = (s32[512,1]{0,1:T(1,128)S(1)}, s32[512,1]{0,1:T(1,128)}, u32[]{:S(2)}) copy-start(s32[512,1]{0,1:T(1,128)} %compare_select_fusion) | copy-start | bytes 6148
  56.3 34.1 %collective-permute-start.8 = (bf16[128,512]{1,0:T(8,128)(2,1)}, bf16[128,512]{1,0:T(8,128)(2,1)}, u32[]{:S(2)}, u32[]{:S(2)}) collective-permute-start(bf16[128,512]{1,0:T(8,128)(2,1)} %get-tuple-element.8), channel_id=1, source_target_pairs={{0,1},{1,2},{2,3},{3,4},{4,5},{5,6},{6,7},{7,8},{8,9},{9,10},{10,1... | collective-permute-start | bytes 393224 | tf_op jit(solution)/shard_map/ppermute | solution.py:21
  56.3 34.1 %collective-permute-start.11 = (bf16[128,512]{1,0:T(8,128)(2,1)}, bf16[128,512]{1,0:T(8,128)(2,1)}, u32[]{:S(2)}, u32[]{:S(2)}) collective-permute-start(bf16[128,512]{1,0:T(8,128)(2,1)} %get-tuple-element.9), channel_id=1, source_target_pairs={{0,126},{1,127},{2,0},{3,1},{4,2},{5,3},{6,4},{7,5},{8,6},{9,7},{1... | collective-permute-start | bytes 393224 | tf_op jit(solution)/shard_map/ppermute | solution.py:21
  64.9 32.3 %collective-permute-start.10 = (bf16[128,512]{1,0:T(8,128)(2,1)}, bf16[128,512]{1,0:T(8,128)(2,1)}, u32[]{:S(2)}, u32[]{:S(2)}) collective-permute-start(bf16[128,512]{1,0:T(8,128)(2,1)} %get-tuple-element.10), channel_id=1, source_target_pairs={{0,2},{1,3},{2,4},{3,5},{4,6},{5,7},{6,8},{7,9},{8,10},{9,11},{10,... | collective-permute-start | bytes 393224 | tf_op jit(solution)/shard_map/ppermute | solution.py:21
  64.9 32.3 %collective-permute-start.9 = (bf16[128,512]{1,0:T(8,128)(2,1)S(1)}, bf16[128,512]{1,0:T(8,128)(2,1)}, u32[]{:S(2)}, u32[]{:S(2)}) collective-permute-start(bf16[128,512]{1,0:T(8,128)(2,1)S(1)} %get-tuple-element.11), channel_id=1, source_target_pairs={{0,127},{1,0},{2,1},{3,2},{4,3},{5,4},{6,5},{7,6},{8,7},{9,8},{10,... | collective-permute-start | bytes 393224 | tf_op jit(solution)/shard_map/ppermute | solution.py:21
  82.4 14.8 %copy-start.6 = (bf16[1024,512]{1,0:T(8,128)(2,1)S(1)}, bf16[1024,512]{1,0:T(8,128)(2,1)}, u32[]{:S(2)}) copy-start(bf16[1024,512]{1,0:T(8,128)(2,1)} %param.9) | copy-start | bytes 3145732
  84.0 20.4 %collective-permute-start.12 = (bf16[128,300]{0,1:T(8,128)(2,1)}, bf16[128,300]{0,1:T(8,128)(2,1)}, u32[]{:S(2)}, u32[]{:S(2)}) collective-permute-start(bf16[128,300]{0,1:T(8,128)(2,1)} %get-tuple-element.20), channel_id=1, source_target_pairs={{0,127},{1,0},{2,1},{3,2},{4,3},{5,4},{6,5},{7,6},{8,7},{9,8},{10,... | collective-permute-start | bytes 230408 | tf_op jit(solution)/shard_map/ppermute | solution.py:34
  90.4 14.1 %collective-permute-start.15 = (bf16[128,300]{0,1:T(8,128)(2,1)}, bf16[128,300]{0,1:T(8,128)(2,1)}, u32[]{:S(2)}, u32[]{:S(2)}) collective-permute-start(bf16[128,300]{0,1:T(8,128)(2,1)} %get-tuple-element.21), channel_id=1, source_target_pairs={{0,2},{1,3},{2,4},{3,5},{4,6},{5,7},{6,8},{7,9},{8,10},{9,11},{10,... | collective-permute-start | bytes 230408 | tf_op jit(solution)/shard_map/ppermute | solution.py:34
  90.4 14.1 %collective-permute-start.14 = (bf16[128,300]{0,1:T(8,128)(2,1)}, bf16[128,300]{0,1:T(8,128)(2,1)}, u32[]{:S(2)}, u32[]{:S(2)}) collective-permute-start(bf16[128,300]{0,1:T(8,128)(2,1)} %get-tuple-element.22), channel_id=1, source_target_pairs={{0,126},{1,127},{2,0},{3,1},{4,2},{5,3},{6,4},{7,5},{8,6},{9,7},{1... | collective-permute-start | bytes 230408 | tf_op jit(solution)/shard_map/ppermute | solution.py:34
  97.3 7.2 %collective-permute-start.13 = (bf16[128,300]{0,1:T(8,128)(2,1)}, bf16[128,300]{0,1:T(8,128)(2,1)}, u32[]{:S(2)}, u32[]{:S(2)}) collective-permute-start(bf16[128,300]{0,1:T(8,128)(2,1)} %get-tuple-element.23), channel_id=1, source_target_pairs={{0,1},{1,2},{2,3},{3,4},{4,5},{5,6},{6,7},{7,8},{8,9},{9,10},{10,1... | collective-permute-start | bytes 230408 | tf_op jit(solution)/shard_map/ppermute | solution.py:34
  (12 other events, 26.9 us)
Sparse Core Ops, SparseCore 0:
  101.0 149.7 all-reduce.2
where the time goes:
time: 262 us; the launch traced here: 261 us
  waiting for transfers between devices  136 us (52%)
  starting transfers between devices  46.3 us (18%)
  local copies, waits for them, and re-layouts  24.8 us (9%)
  matrix products  20.8 us (8%)
  other arithmetic  19.1 us (7%)
  between operations  14.3 us (5%)
    psum x1, waiting for transfers between devices, device_step(): dw_first = lax.psum(contract_rows(z_first, grad_pre), 'nodes')  136 us
    ppermute x8, starting transfers between devices, aggregate_back(): lax.ppermute(outward[link * num_slots:(link + 1) * num_slots], 'nodes', s...  26.5 us
    ppermute x8, starting transfers between devices, halo_rows(): lax.ppermute(sent_rows[link], 'nodes', shift_pairs(axis_size, offset))  19.8 us
    scatter-add x2, other arithmetic, aggregate_back(): return inner_sum.at[send_idx.reshape(-1)].add(returned)  13.5 us
    dot_general x6, matrix products, contract_rows(): lax.dot_general(left_rows, right_rows, (((0,), (0,)), ((), ())), preferre...  12.6 us
    unnamed x42, local copies, waits for them, and re-layouts  9.77 us
  transfers between devices with their start and end apart: 17, of which 1 were waited for; matrix products, arithmetic and copies ran while one was open for 20% of the time, Pallas kernels for 0%

commit v1 on v0

v1 whole, which is shorter than its diff:
```python
import jax
import jax.numpy as jnp
from jax import lax
from jax.experimental import pallas as pl
from jax.experimental.pallas import tpu as pltpu
from jax.sharding import PartitionSpec as P

F32 = jnp.float32
BF16 = jnp.bfloat16
NX, NY, NZ = 4, 4, 4
PLANE = NY * NZ
OFFSETS = (1, -1, 2, -2)
LINKS = 4


def dot(a, b, ca, cb):
    return lax.dot_general(a, b, (((ca,), (cb,)), ((), ())), preferred_element_type=F32)


def build(n_dev, nodes, feat, hid, cls, slots):
    all_slots = LINKS * slots
    slab1 = (feat + 7) // 8 * 8
    slab2 = (cls + 7) // 8 * 8
    n_slab = hid // 128
    half_slabs = n_slab // 2
    used = half_slabs * (slab1 + slab2)
    chunk = -(-used // (PLANE * 8)) * 8
    half = chunk * PLANE
    off2 = half_slabs * slab1

    def kernel(h0_hbm, aint_hbm, ahalo_hbm, idx_hbm, w0_hbm, w1_hbm, g_hbm,
               dw1_out, dw2_out, gf_hbm,
               h0, aint, ahalo, idx, w0, w1, g,
               pt, e1, z0, ft, e0,
               s0, halo0, o1, r1, sz, haloz, o0, r0,
               z0acc, d1acc, z1acc, gfacc,
               part, pair_in, rs_in, x_in, res,
               in_sem, out_sem, fwd_s, fwd_r, bwd_s, bwd_r, zs, zr, os_, or_,
               pair_s, pair_r, rs_s, rs_r, x_s, x_r, ag_s, ag_r, back_s, back_r):
        me = lax.axis_index("nodes")
        core = lax.rem(me, 2)
        x = lax.rem(me // 2, NX)
        plane = me // (2 * NX)

        def dev(i):
            return {"nodes": i}

        def plane_dev(i):
            return i * (2 * NX) + x * 2 + core

        def x_dev(i):
            return plane * (2 * NX) + i * 2 + core

        def near(o):
            return lax.rem(me + (o + n_dev), n_dev)

        mate = me + 1 - 2 * core

        loads = [pltpu.make_async_copy(a, b, in_sem.at[i]) for i, (a, b) in enumerate((
            (idx_hbm, idx), (h0_hbm, h0), (g_hbm, g), (w1_hbm, w1), (ahalo_hbm, ahalo), (aint_hbm, aint), (w0_hbm, w0)))]
        for cp in loads:
            cp.start()
        ld_idx, ld_h0, ld_g, ld_w1, ld_ahalo, ld_aint, ld_w0 = loads

        barrier = pltpu.get_barrier_semaphore()

        def sig(d):
            pl.semaphore_signal(barrier, inc=1, device_id=dev(d), device_id_type=pl.DeviceIdType.MESH)

        for o in OFFSETS:
            sig(near(o))
        sig(mate)

        def sig_x(p, c):
            sig(x_dev(lax.rem(x + p, NX)))
            return c

        def sig_p(p, c):
            sig(plane_dev(lax.rem(plane + p, PLANE)))
            return c

        lax.fori_loop(1, NX, sig_x, 0)
        lax.fori_loop(1, PLANE, sig_p, 0)

        def rcopy(src, dst, ss, rs, d):
            return pltpu.make_async_remote_copy(src_ref=src, dst_ref=dst, send_sem=ss, recv_sem=rs,
                                                device_id=dev(d), device_id_type=pl.DeviceIdType.MESH)

        def lanes(ref, k):
            return ref.at[:, pl.ds(k * slots, slots)]

        def link_copies(src, dst, ss, rs, sign):
            return [rcopy(lanes(src, k), lanes(dst, k), ss.at[k], rs.at[k], near(sign * OFFSETS[k])) for k in range(LINKS)]

        ld_idx.wait()
        rows = lax.broadcasted_iota(jnp.int32, (nodes, slots), 0)
        for k in range(LINKS):
            pt[:, k * slots:(k + 1) * slots] = jnp.where(rows == idx[k:k + 1, :], 1.0, 0.0).astype(BF16)
        ld_h0.wait()
        s0[...] = dot(h0[...], pt[...], 1, 0).astype(BF16)

        pl.semaphore_wait(barrier, LINKS + 1 + (NX - 1) + (PLANE - 1))
        fwd = link_copies(s0, halo0, fwd_s, fwd_r, 1)
        for cp in fwd:
            cp.start()

        ld_g.wait()
        ld_w1.wait()
        e1[...] = dot(w1[...], g[...], 0, 0).astype(BF16)
        ld_ahalo.wait()
        o1[...] = dot(e1[...], ahalo[...], 1, 0).astype(BF16)
        bwd = link_copies(o1, r1, bwd_s, bwd_r, -1)
        for cp in bwd:
            cp.start()

        ld_aint.wait()
        ld_w0.wait()
        z0acc[...] = dot(h0[...], aint[...], 1, 1)
        d1acc[...] = dot(e1[...], aint[...], 1, 0)

        for cp in fwd:
            cp.wait()
        z0[...] = (z0acc[...] + dot(halo0[...], ahalo[...], 1, 1)).astype(BF16)
        sz[...] = dot(z0[...], pt[...], 1, 0).astype(BF16)
        zcp = link_copies(sz, haloz, zs, zr, 1)
        for cp in zcp:
            cp.start()
        h1 = jnp.maximum(dot(w0[...], z0[...], 0, 0), 0.0).astype(BF16)
        ft[...] = h1
        z1acc[...] = dot(ft[...], aint[...], 1, 1)

        for cp in bwd:
            cp.wait()
        d1 = d1acc[...] + dot(r1[...], pt[...], 1, 1)
        ft[...] = jnp.where(ft[...] > 0, d1, 0.0).astype(BF16)

        part[...] = jnp.zeros_like(part)
        dw1 = dot(z0[...], ft[...], 1, 1)
        for s in range(n_slab):
            part[s // half_slabs, pl.ds((s % half_slabs) * slab1, feat), :] = dw1[:, s * 128:(s + 1) * 128]

        e0[...] = dot(w0[...], ft[...], 1, 0).astype(BF16)
        o0[...] = dot(e0[...], ahalo[...], 1, 0).astype(BF16)
        ocp = link_copies(o0, r0, os_, or_, -1)
        for cp in ocp:
            cp.start()

        for cp in zcp:
            cp.wait()
        h1h = jnp.maximum(dot(w0[...], haloz[...], 0, 0), 0.0).astype(BF16)
        z1 = (z1acc[...] + dot(h1h, ahalo[...], 1, 1)).astype(BF16)
        dw2 = dot(g[...], z1, 1, 1)
        for s in range(n_slab):
            part[s // half_slabs, pl.ds(off2 + (s % half_slabs) * slab2, cls), :] = dw2[:, s * 128:(s + 1) * 128]

        pair = rcopy(part.at[1 - core], pair_in, pair_s, pair_r, mate)
        pair.start()
        gfacc[...] = dot(e0[...], aint[...], 1, 0)
        pair.wait()
        part[core] = part[core] + pair_in[...]

        def rs_copy(p):
            i = lax.rem(plane + p, PLANE)
            return rcopy(part.at[core, pl.ds(pl.multiple_of(i * chunk, 8), chunk), :], rs_in.at[plane], rs_s.at[i], rs_r.at[plane], plane_dev(i))

        def rs_start(p, c):
            rs_copy(p).start()
            return c

        lax.fori_loop(1, PLANE, rs_start, 0)

        for cp in ocp:
            cp.wait()
        gfacc[...] = gfacc[...] + dot(r0[...], pt[...], 1, 1)
        gf_out = pltpu.make_async_copy(gfacc, gf_hbm, out_sem)
        gf_out.start()

        rs_in[plane] = part[core, pl.ds(pl.multiple_of(plane * chunk, 8), chunk), :]

        def rs_wait(p, c):
            i = lax.rem(plane + p, PLANE)
            cp = rcopy(part.at[core, pl.ds(pl.multiple_of(i * chunk, 8), chunk), :], rs_in.at[i], rs_s.at[i], rs_r.at[i], plane_dev(i))
            cp.wait()
            return c

        lax.fori_loop(1, PLANE, rs_wait, 0)
        total = rs_in[0]
        for i in range(1, PLANE):
            total = total + rs_in[i]
        x_in[x] = total

        def x_copy(i):
            return rcopy(x_in.at[x], x_in.at[x], x_s.at[i], x_r.at[x], x_dev(i))

        def x_start(p, c):
            x_copy(lax.rem(x + p, NX)).start()
            return c

        def x_wait(p, c):
            i = lax.rem(x + p, NX)
            rcopy(x_in.at[x], x_in.at[i], x_s.at[i], x_r.at[i], x_dev(i)).wait()
            return c

        lax.fori_loop(1, NX, x_start, 0)
        lax.fori_loop(1, NX, x_wait, 0)
        final = x_in[0]
        for i in range(1, NX):
            final = final + x_in[i]

        def own(i):
            return res.at[core, pl.ds(pl.multiple_of(i * chunk, 8), chunk), :]

        res[core, pl.ds(pl.multiple_of(plane * chunk, 8), chunk), :] = final

        def ag_start(p, c):
            i = lax.rem(plane + p, PLANE)
            rcopy(own(plane), own(plane), ag_s.at[i], ag_r.at[plane], plane_dev(i)).start()
            return c

        def ag_wait(p, c):
            i = lax.rem(plane + p, PLANE)
            rcopy(own(plane), own(i), ag_s.at[i], ag_r.at[i], plane_dev(i)).wait()
            return c

        lax.fori_loop(1, PLANE, ag_start, 0)
        lax.fori_loop(1, PLANE, ag_wait, 0)
        back = rcopy(res.at[core], res.at[core], back_s, back_r, mate)
        back.start()
        back_in = rcopy(res.at[core], res.at[1 - core], back_s, back_r, mate)
        back_in.wait()
        for s in range(n_slab):
            h, q = s // half_slabs, s % half_slabs
            dw1_out[:, s * 128:(s + 1) * 128] = res[h, pl.ds(q * slab1, feat), :]
            dw2_out[:, s * 128:(s + 1) * 128] = res[h, pl.ds(off2 + q * slab2, cls), :]
        gf_out.wait()

    V = pltpu.VMEM
    D = pltpu.SemaphoreType.DMA
    scratch = [
        V((feat, nodes), BF16), V((nodes, nodes), BF16), V((nodes, all_slots), BF16), V((LINKS, slots), jnp.int32),
        V((feat, hid), BF16), V((cls, hid), BF16), V((cls, nodes), BF16),
        V((nodes, all_slots), BF16), V((hid, nodes), BF16), V((feat, nodes), BF16), V((hid, nodes), BF16), V((feat, nodes), BF16),
        V((feat, all_slots), BF16), V((feat, all_slots), BF16), V((hid, all_slots), BF16), V((hid, all_slots), BF16),
        V((feat, all_slots), BF16), V((feat, all_slots), BF16), V((feat, all_slots), BF16), V((feat, all_slots), BF16),
        V((feat, nodes), F32), V((hid, nodes), F32), V((hid, nodes), F32), V((feat, nodes), F32),
        V((2, half, 128), F32), V((half, 128), F32), V((PLANE, chunk, 128), F32), V((NX, chunk, 128), F32), V((2, half, 128), F32),
        D((7,)), D, D((LINKS,)), D((LINKS,)), D((LINKS,)), D((LINKS,)), D((LINKS,)), D((LINKS,)), D((LINKS,)), D((LINKS,)),
        D, D, D((PLANE,)), D((PLANE,)), D((NX,)), D((NX,)), D((PLANE,)), D((PLANE,)), D, D,
    ]
    any_spec = pl.BlockSpec(memory_space=pl.ANY)
    vmem_spec = pl.BlockSpec(memory_space=pltpu.VMEM)
    return pl.pallas_call(
        kernel,
        out_shape=(jax.ShapeDtypeStruct((feat, hid), F32), jax.ShapeDtypeStruct((cls, hid), F32), jax.ShapeDtypeStruct((feat, nodes), F32)),
        in_specs=[any_spec] * 7,
        out_specs=(vmem_spec, vmem_spec, any_spec),
        scratch_shapes=scratch,
        compiler_params=pltpu.CompilerParams(collective_id=0, has_side_effects=True, vmem_limit_bytes=60 * 1024 * 1024),
        name="gcn_backward",
    )


def solution(mesh):
    axis_size = mesh.shape["nodes"]
    row_spec = P(("graph", "nodes"), None)
    replicated = P(None, None)
    part_spec = P("graph", None)

    def device_step(node_feats, a_int, a_halo, send_idx, w_first, w_second, grad_out):
        nodes, feat = node_feats.shape
        hid, cls = w_second.shape
        call = build(axis_size, nodes, feat, hid, cls, send_idx.shape[1])
        dw1, dw2, gf = call(node_feats.T, a_int, a_halo, send_idx, w_first, w_second.T, grad_out.T)
        return dw1, dw2.T, gf.T

    return jax.shard_map(device_step, mesh=mesh, in_specs=(row_spec, row_spec, row_spec, row_spec, replicated, replicated, row_spec), out_specs=(part_spec, part_spec, row_spec), check_vma=False)
```

time: 262 us -> 54.6 us (0.21)
  waiting for transfers between devices: 136 us -> 0 us
  Pallas kernels: 0 us -> 49.1 us
  starting transfers between devices: 46.3 us -> 0 us
  matrix products: 20.8 us -> 0 us
  local copies, waits for them, and re-layouts: 24.8 us -> 4.71 us
  other arithmetic: 19.1 us -> 0 us
  between operations: 14.3 us -> 0.65 us
    psum x1 -> x0, waiting for transfers between devices: 136 us -> none  [device_step(): dw_first = lax.psum(contract_rows(z_first, grad_pre), 'nodes')]
    pallas_call x0 -> x1, Pallas kernels: none -> 49.1 us  [device_step(): call(node_feats.T, a_int, a_halo, send_idx, w_first, w_second.T, grad_out.T)]
    ppermute x16 -> x0, starting transfers between devices: 46.3 us -> none  [the longest x8 26.5 us: aggregate_back(): lax.ppermute(outward[link * num_slots:(link + 1) * num_slots], 'nodes', s...]
    dot_general x12 -> x0, matrix products: 20.8 us -> none  [the longest x6 12.6 us: contract_rows(): lax.dot_general(left_rows, right_rows, (((0,), (0,)), ((), ())), preferre...]
    scatter-add x2 -> x0, other arithmetic: 13.5 us -> none  [aggregate_back(): return inner_sum.at[send_idx.reshape(-1)].add(returned)]
    unnamed x42 -> x5, local copies, waits for them, and re-layouts: 9.77 us -> 4.71 us
    gather x2 -> x0, local copies, waits for them, and re-layouts: 4.56 us -> none  [halo_rows(): sent_rows = jnp.take(features, send_idx, axis=0)]
    dot_general x2 -> x0, local copies, waits for them, and re-layouts: 4.54 us -> none  [contract_rows(): lax.dot_general(left_rows, right_rows, (((0,), (0,)), ((), ())), preferre...]
  transfers between devices with their start and end apart: 17 -> 0, of which waited for: 1 -> 0; matrix products, arithmetic and copies ran while one was open for 20% -> 0% of each run, Pallas kernels for 0% -> 0%
where the time goes in v1:
time: 54.6 us; the launch traced here: 54.5 us
  Pallas kernels  49.1 us (90%)
  local copies, waits for them, and re-layouts  4.71 us (9%)
  between operations  0.65 us (1%)
    pallas_call x1, Pallas kernels, device_step(): call(node_feats.T, a_int, a_halo, send_idx, w_first, w_second.T, grad_out.T)  49.1 us
    unnamed x5, local copies, waits for them, and re-layouts  4.71 us

profile of v1, /device:TPU:1, one launch (start us, length us, event | category | flops | bytes accessed | tf_op | source)
XLA Modules:
  0.0 54.5 jit_solution(6823836859475762575)
XLA Ops:
  0.6 49.1 %gcn_backward.1 = (f32[300,512]{1,0:T(8,128)}, f32[100,512]{1,0:T(8,128)}, f32[300,1024]{1,0:T(8,128)}) custom-call(bf16[300,1024]{1,0:T(8,128)(2,1)} %bitcast.6, bf16[1024,1024]{1,0:T(8,128)(2,1)} %aint_hbm.1, bf16[1024,512]{1,0:T(8,128)(2,1)} %ahalo_hbm.1, s32[4,128]{1,0:T(4,128)} %idx_hbm.1, bf16[300,512]{1,0:T(8,128)(2,1)} %w0_hbm.1, ...), custom_call_target="tpu_custom_call" | custom-call | tf_op jit(solution)/shard_map/gcn_backward/pallas_call | solution.py:273
  49.8 0.0 copy-start
  49.8 2.0 %copy.13 = f32[300,512]{1,0:T(8,128)} copy(f32[300,512]{1,0:T(8,128)} %get-tuple-element.12) | data formatting | bytes 1228800
  51.8 1.6 %copy.14 = f32[512,100]{0,1:T(8,128)} copy(f32[512,100]{0,1:T(8,128)} %bitcast.7) | data formatting | bytes 409600
  53.4 0.0 copy-done
  53.4 1.0 %copy.15 = f32[1024,300]{0,1:T(8,128)} copy(f32[1024,300]{0,1:T(8,128)S(1)} %bitcast.5) | data formatting | bytes 2457600
Async XLA Ops:
  49.8 3.7 %copy-start = (f32[300,1024]{1,0:T(8,128)S(1)}, f32[300,1024]{1,0:T(8,128)}, u32[]{:S(2)}) copy-start(f32[300,1024]{1,0:T(8,128)} %get-tuple-element.8) | copy-start | bytes 3686404

commit v2 on v1

--- a/solution.py
+++ b/solution.py
@@ -29,13 +29,13 @@
     off2 = half_slabs * slab1
 
     def kernel(h0_hbm, aint_hbm, ahalo_hbm, idx_hbm, w0_hbm, w1_hbm, g_hbm,
-               dw1_out, dw2_out, gf_hbm,
+               dw1_out, dw2_out, gf_out,
                h0, aint, ahalo, idx, w0, w1, g,
                pt, e1, z0, ft, e0,
                s0, halo0, o1, r1, sz, haloz, o0, r0,
                z0acc, d1acc, z1acc, gfacc,
                part, pair_in, rs_in, x_in, res,
-               in_sem, out_sem, fwd_s, fwd_r, bwd_s, bwd_r, zs, zr, os_, or_,
+               in_sem, fwd_s, fwd_r, bwd_s, bwd_r, zs, zr, os_, or_,
                pair_s, pair_r, rs_s, rs_r, x_s, x_r, ag_s, ag_r, back_s, back_r):
         me = lax.axis_index("nodes")
         core = lax.rem(me, 2)
@@ -171,9 +171,7 @@
 
         for cp in ocp:
             cp.wait()
-        gfacc[...] = gfacc[...] + dot(r0[...], pt[...], 1, 1)
-        gf_out = pltpu.make_async_copy(gfacc, gf_hbm, out_sem)
-        gf_out.start()
+        gf_out[...] = gfacc[...] + dot(r0[...], pt[...], 1, 1)
 
         rs_in[plane] = part[core, pl.ds(pl.multiple_of(plane * chunk, 8), chunk), :]
 
@@ -232,7 +230,6 @@
             h, q = s // half_slabs, s % half_slabs
             dw1_out[:, s * 128:(s + 1) * 128] = res[h, pl.ds(q * slab1, feat), :]
             dw2_out[:, s * 128:(s + 1) * 128] = res[h, pl.ds(off2 + q * slab2, cls), :]
-        gf_out.wait()
 
     V = pltpu.VMEM
     D = pltpu.SemaphoreType.DMA
@@ -244,19 +241,38 @@
         V((feat, all_slots), BF16), V((feat, all_slots), BF16), V((feat, all_slots), BF16), V((feat, all_slots), BF16),
         V((feat, nodes), F32), V((hid, nodes), F32), V((hid, nodes), F32), V((feat, nodes), F32),
         V((2, half, 128), F32), V((half, 128), F32), V((PLANE, chunk, 128), F32), V((NX, chunk, 128), F32), V((2, half, 128), F32),
-        D((7,)), D, D((LINKS,)), D((LINKS,)), D((LINKS,)), D((LINKS,)), D((LINKS,)), D((LINKS,)), D((LINKS,)), D((LINKS,)),
+        D((7,)), D((LINKS,)), D((LINKS,)), D((LINKS,)), D((LINKS,)), D((LINKS,)), D((LINKS,)), D((LINKS,)), D((LINKS,)),
         D, D, D((PLANE,)), D((PLANE,)), D((NX,)), D((NX,)), D((PLANE,)), D((PLANE,)), D, D,
     ]
     any_spec = pl.BlockSpec(memory_space=pl.ANY)
     vmem_spec = pl.BlockSpec(memory_space=pltpu.VMEM)
     return pl.pallas_call(
         kernel,
+        out_shape=(pltpu.VMEM((feat, hid), F32), pltpu.VMEM((cls, hid), F32), pltpu.VMEM((feat, nodes), F32)),
+        in_specs=[any_spec] * 7,
+        out_specs=(vmem_spec, vmem_spec, vmem_spec),
+        scratch_shapes=scratch,
+        compiler_params=pltpu.CompilerParams(collective_id=0, has_side_effects=True, vmem_limit_bytes=64897024),
+        name="gcn_backward",
+    )
+
+
+def write_out(feat, hid, cls, nodes):
+    def kernel(dw1, dw2, gf, dw1_out, dw2_out, gf_out, sems):
+        copies = [pltpu.make_async_copy(a, b, sems.at[i]) for i, (a, b) in enumerate(((gf, gf_out), (dw1, dw1_out), (dw2, dw2_out)))]
+        for cp in copies:
+            cp.start()
+        for cp in copies:
+            cp.wait()
+
+    return pl.pallas_call(
+        kernel,
         out_shape=(jax.ShapeDtypeStruct((feat, hid), F32), jax.ShapeDtypeStruct((cls, hid), F32), jax.ShapeDtypeStruct((feat, nodes), F32)),
-        in_specs=[any_spec] * 7,
-        out_specs=(vmem_spec, vmem_spec, any_spec),
-        scratch_shapes=scratch,
-        compiler_params=pltpu.CompilerParams(collective_id=0, has_side_effects=True, vmem_limit_bytes=60 * 1024 * 1024),
-        name="gcn_backward",
+        in_specs=[pl.BlockSpec(memory_space=pltpu.VMEM)] * 3,
+        out_specs=(pl.BlockSpec(memory_space=pl.ANY),) * 3,
+        scratch_shapes=[pltpu.SemaphoreType.DMA((3,))],
+        compiler_params=pltpu.CompilerParams(vmem_limit_bytes=4 * 1024 * 1024),
+        name="write_out",
     )
 
 
@@ -271,6 +287,7 @@
         hid, cls = w_second.shape
         call = build(axis_size, nodes, feat, hid, cls, send_idx.shape[1])
         dw1, dw2, gf = call(node_feats.T, a_int, a_halo, send_idx, w_first, w_second.T, grad_out.T)
+        dw1, dw2, gf = write_out(feat, hid, cls, nodes)(dw1, dw2, gf)
         return dw1, dw2.T, gf.T
 
     return jax.shard_map(device_step, mesh=mesh, in_specs=(row_spec, row_spec, row_spec, row_spec, replicated, replicated, row_spec), out_specs=(part_spec, part_spec, row_spec), check_vma=False)

time: 54.6 us -> 50.2 us (0.919)
  local copies, waits for them, and re-layouts: 4.71 us -> 0 us
    unnamed x5 -> x0, local copies, waits for them, and re-layouts: 4.71 us -> none
    pallas_call x0 -> x1, Pallas kernels: none -> 1.33 us  [device_step(): dw1, dw2, gf = write_out(feat, hid, cls, nodes)(dw1, dw2, gf)]
    pallas_call x1, Pallas kernels: 49.1 us -> 48.2 us  [device_step(): call(node_feats.T, a_int, a_halo, send_idx, w_first, w_second.T, grad_out.T)]
where the time goes in v2:
time: 50.2 us; the launch traced here: 50.1 us
  Pallas kernels  49.5 us (99%)
  between operations  0.64 us (1%)
    pallas_call x1, Pallas kernels, device_step(): call(node_feats.T, a_int, a_halo, send_idx, w_first, w_second.T, grad_out.T)  48.2 us
    pallas_call x1, Pallas kernels, device_step(): dw1, dw2, gf = write_out(feat, hid, cls, nodes)(dw1, dw2, gf)  1.33 us

profile of v2, /device:TPU:1, one launch (start us, length us, event | category | flops | bytes accessed | tf_op | source)
XLA Modules:
  0.0 50.1 jit_solution(16167101513942560138)
XLA Ops:
  0.6 48.2 %gcn_backward.1 = (f32[300,512]{1,0:T(8,128)S(1)}, f32[100,512]{1,0:T(8,128)S(1)}, f32[300,1024]{1,0:T(8,128)S(1)}) custom-call(bf16[300,1024]{1,0:T(8,128)(2,1)} %bitcast.5, bf16[1024,1024]{1,0:T(8,128)(2,1)} %aint_hbm.1, bf16[1024,512]{1,0:T(8,128)(2,1)} %ahalo_hbm.1, s32[4,128]{1,0:T(4,128)} %idx_hbm.1, bf16[300,512]{1,0:T(8,128)(2,1)} %w0_hbm.1, ...), custom_call_target="tpu_custom_call" | custom-call | tf_op jit(solution)/shard_map/gcn_backward/pallas_call | solution.py:289
  48.8 1.3 %write_out.1 = (f32[300,512]{1,0:T(8,128)}, f32[100,512]{1,0:T(8,128)}, f32[300,1024]{1,0:T(8,128)}) custom-call(f32[300,512]{1,0:T(8,128)S(1)} %get-tuple-element.9.dw1, f32[100,512]{1,0:T(8,128)S(1)} %get-tuple-element.10.dw2, f32[300,1024]{1,0:T(8,128)S(1)} %get-tuple-element.11.gf), custom_call_target="tpu_custom_call" | custom-call | tf_op jit(solution)/shard_map/write_out/pallas_call | solution.py:290

commit v3 on v0

v3 whole, which is shorter than its diff:
```python
import jax
import jax.numpy as jnp
from jax import lax
from jax.experimental import pallas as pl
from jax.experimental.pallas import tpu as pltpu
from jax.sharding import PartitionSpec as P

F32 = jnp.float32
BF16 = jnp.bfloat16
SIDE = 4
PLANE = SIDE * SIDE
CUBE = PLANE * SIDE
OFFSETS = (1, -1, 2, -2)
LINKS = 4
VMEM_BYTES = 67043328


def dot(a, b, ca, cb):
    return lax.dot_general(a, b, (((ca,), (cb,)), ((), ())), preferred_element_type=F32)


def hops(step):
    return sum(min(d, SIDE - d) for d in step)


PLANE_PEERS = sorted(((a, b) for a in range(SIDE) for b in range(SIDE) if a or b), key=hops, reverse=True)
CUBE_PEERS = sorted(((a, b, c) for a in range(SIDE) for b in range(SIDE) for c in range(SIDE) if a or b or c), key=hops, reverse=True)


class Piece:
    def __init__(self, num, plane, cross, rows, base):
        self.num, self.plane, self.cross, self.rows, self.base = num, plane, cross, rows, base

    def steps(self, ab):
        st = [0, 0, 0]
        st[self.plane[0]], st[self.plane[1]] = ab
        return tuple(st)

    def across(self, step):
        st = [0, 0, 0]
        st[self.cross] = step
        return tuple(st)


def build(n_dev, nodes, feat, hid, cls, slots):
    all_slots = LINKS * slots
    half_hid = hid // 2
    n_slab = hid // 128
    slab1 = (feat + 7) // 8 * 8
    slab2 = (cls + 7) // 8 * 8
    half_rows = n_slab // 2 * slab1
    units = -(-half_rows // (PLANE * 8))
    share = [8 * ((units + 2 - p) // 3) for p in range(3)]
    pieces, end1 = [], 0
    for num, (dims, rows) in enumerate(zip((((1, 2), 0), ((0, 1), 2), ((0, 2), 1)), share)):
        pieces.append(Piece(num, dims[0], dims[1], rows, end1))
        end1 += rows * PLANE
    rows1 = sum(share)
    rows2 = -(-n_slab * slab2 // (CUBE * 8)) * 8
    end2 = rows2 * CUBE

    def kernel(h0_hbm, aint_hbm, ahalo_hbm, idx_hbm, w0_hbm, w1_hbm, g_hbm,
               dw1_out, dw2_out, gf_out,
               h0, aint, ahalo, idx, w0, w1, g,
               pt, e1, z0, ft, e0,
               s0, halo0, o1, r1, sz, haloz, o0, r0,
               z0acc, d1acc, z1acc, gfacc,
               part1, part2, pair1_in, pair2_in, rs1_in, rs2_in, x_in, res1, res2,
               in_sem, fwd_sem, bwd_sem, zcp_sem, ocp_sem,
               pair1_sem, pair2_sem, rs1_sem, rs2_sem, x_sem, ag1_s, ag1_r, ag2_s, ag2_r, back1_sem, back2_sem, gossip):
        me = lax.axis_index("nodes")
        core = lax.rem(me, 2)
        coord = (lax.rem(me // 2, SIDE), lax.rem(me // (2 * SIDE), SIDE), me // (2 * SIDE * SIDE))
        stride = (2, 2 * SIDE, 2 * SIDE * SIDE)
        mate = me + 1 - 2 * core

        def moved(dim, step):
            return lax.rem(coord[dim] + step, SIDE)

        def peer(steps):
            d = core
            for dim in range(3):
                d = d + moved(dim, steps[dim]) * stride[dim]
            return d

        def near(o):
            return lax.rem(me + (o + n_dev), n_dev)

        def signal(sem, d):
            pl.semaphore_signal(sem, inc=1, device_id={"nodes": d}, device_id_type=pl.DeviceIdType.MESH)

        def rcopy(src, dst, ss, rs, d):
            return pltpu.make_async_remote_copy(src_ref=src, dst_ref=dst, send_sem=ss, recv_sem=rs,
                                                device_id={"nodes": d}, device_id_type=pl.DeviceIdType.MESH)

        def lanes(ref, k):
            return ref.at[:, pl.ds(k * slots, slots)]

        def link_copies(src, dst, sems, sign):
            return [rcopy(lanes(src, k), lanes(dst, k), sems.at[0, k // 2], sems.at[1, k // 2], near(sign * OFFSETS[k])) for k in range(LINKS)]

        def link_wait(src, dst, sems, i):
            both = pl.ds(2 * i * slots, 2 * slots)
            rcopy(src.at[:, both], dst.at[:, both], sems.at[0, i], sems.at[1, i], mate).wait()

        def start(copies):
            for cp in copies:
                cp.start()

        def wait(copies):
            for cp in copies:
                cp.wait()

        loads = [pltpu.make_async_copy(a, b, in_sem.at[i]) for i, (a, b) in enumerate((
            (idx_hbm, idx), (h0_hbm, h0), (g_hbm, g), (w1_hbm, w1), (ahalo_hbm, ahalo), (aint_hbm, aint), (w0_hbm, w0)))]
        start(loads)
        ld_idx, ld_h0, ld_g, ld_w1, ld_ahalo, ld_aint, ld_w0 = loads
        barrier = pltpu.get_barrier_semaphore()
        ring = [peer(tuple(step if d == dim else 0 for d in range(3))) for dim in range(3) for step in (1, SIDE - 1)]
        greeted = [near(o) for o in OFFSETS] + [mate] + ring
        for d in greeted:
            signal(barrier, d)

        def gossip_send(i):
            for d in ring:
                signal(gossip.at[i], d)

        def gossip_wait(i):
            pl.semaphore_wait(gossip.at[i], len(ring))

        part1[...] = jnp.zeros_like(part1)
        part2[...] = jnp.zeros_like(part2)
        node_id = lax.broadcasted_iota(jnp.int32, (nodes, slots), 0)
        fwd = link_copies(s0, halo0, fwd_sem, 1)
        bwd = link_copies(o1, r1, bwd_sem, -1)
        zcp = link_copies(sz, haloz, zcp_sem, 1)
        ocp = link_copies(o0, r0, ocp_sem, -1)
        upper = pl.ds(2 * slots, 2 * slots)
        lower = pl.ds(0, 2 * slots)

        def select_rows(ks):
            for k in ks:
                pt[:, k * slots:(k + 1) * slots] = jnp.where(node_id == idx[k:k + 1, :], 1.0, 0.0).astype(BF16)

        with jax.named_scope("ld_idx"):
            ld_idx.wait()
        with jax.named_scope("pt"):
            select_rows((2, 3))
        with jax.named_scope("ld_h0"):
            ld_h0.wait()
        with jax.named_scope("s0"):
            s0[:, upper] = dot(h0[...], pt[:, upper], 1, 0).astype(BF16)
        with jax.named_scope("barrier"):
            pl.semaphore_wait(barrier, len(greeted))
        with jax.named_scope("fwd_start"):
            start(fwd[2:])
        with jax.named_scope("s0_low"):
            select_rows((0, 1))
            s0[:, lower] = dot(h0[...], pt[:, lower], 1, 0).astype(BF16)
        with jax.named_scope("fwd_start_low"):
            start(fwd[:2])
            gossip_send(0)
        with jax.named_scope("e1"):
            ld_g.wait()
            ld_w1.wait()
            e1[...] = dot(w1[...], g[...], 0, 0).astype(BF16)
        with jax.named_scope("o1"):
            ld_ahalo.wait()
            o1[...] = dot(e1[...], ahalo[...], 1, 0).astype(BF16)
        with jax.named_scope("bwd_start"):
            start(bwd[2:] + bwd[:2])
        with jax.named_scope("z0acc"):
            ld_aint.wait()
            z0acc[...] = dot(h0[...], aint[...], 1, 1)
        with jax.named_scope("gossip0"):
            gossip_wait(0)
            gossip_send(1)
        with jax.named_scope("d1acc"):
            d1acc[...] = dot(e1[...], aint[...], 1, 0)

        with jax.named_scope("fwd_wait"):
            link_wait(s0, halo0, fwd_sem, 0)
            link_wait(s0, halo0, fwd_sem, 1)
        with jax.named_scope("z0"):
            z0[...] = (z0acc[...] + dot(halo0[...], ahalo[...], 1, 1)).astype(BF16)
        with jax.named_scope("sz"):
            sz[...] = dot(z0[...], pt[...], 1, 0).astype(BF16)
        with jax.named_scope("z_start"):
            start(zcp[2:] + zcp[:2])
        with jax.named_scope("gossip1"):
            gossip_wait(1)
            gossip_send(2)
        with jax.named_scope("h1"):
            ld_w0.wait()
            ft[...] = jnp.maximum(dot(w0[...], z0[...], 0, 0), 0.0).astype(BF16)
        with jax.named_scope("z1acc"):
            z1acc[...] = dot(ft[...], aint[...], 1, 1)
        with jax.named_scope("gossip2"):
            gossip_wait(2)
            gossip_send(3)

        with jax.named_scope("bwd_wait_up"):
            link_wait(o1, r1, bwd_sem, 1)
        with jax.named_scope("d1_up"):
            d1acc[...] = d1acc[...] + dot(r1[:, upper], pt[:, upper], 1, 1)
        with jax.named_scope("bwd_wait_low"):
            link_wait(o1, r1, bwd_sem, 0)

        def first_half(h):
            rows = pl.ds(pl.multiple_of(h * half_hid, half_hid), half_hid)
            d1 = d1acc[rows, :] + dot(r1[rows, lower], pt[:, lower], 1, 1)
            ft[rows, :] = jnp.where(ft[rows, :] > 0, d1, 0.0).astype(BF16)
            dw1 = dot(z0[...], ft[rows, :], 1, 1)
            for s in range(half_hid // 128):
                part1[h, pl.ds(s * slab1, feat), :] = dw1[:, s * 128:(s + 1) * 128]

        def rows_of(ref, n, i):
            return ref.at[pl.ds(pl.multiple_of(i * n, 8), n), :]

        def rows_wait(ref, rows, ss, rs):
            some = ref.at[pl.ds(0, rows), :]
            if ss is not None:
                rcopy(some, some, ss, ss, mate).wait_send()
            if rs is not None:
                rcopy(some, some, rs, rs, mate).wait_recv()

        pair1 = rcopy(part1.at[1 - core, pl.ds(0, half_rows), :], pair1_in, pair1_sem.at[0], pair1_sem.at[1], mate)

        def plane_id(p, ab=(0, 0)):
            return moved(p.plane[0], ab[0]) * SIDE + moved(p.plane[1], ab[1])

        def chunk1(ref, p, i):
            return ref.at[core, pl.ds(pl.multiple_of(p.base + i * p.rows, 8), p.rows), :]

        def stage(ref, p, i):
            return ref.at[p.num, i, pl.ds(0, p.rows), :]

        def rs1_send(group):
            start([rcopy(chunk1(part1, p, plane_id(p, ab)), stage(rs1_in, p, plane_id(p)), rs1_sem.at[0], rs1_sem.at[1], peer(p.steps(ab)))
                   for ab in PLANE_PEERS for p in group])
            for p in group:
                rs1_in[p.num, plane_id(p), pl.ds(0, p.rows), :] = part1[core, pl.ds(pl.multiple_of(p.base + plane_id(p) * p.rows, 8), p.rows), :]

        def rs1_start():
            used = pl.ds(0, half_rows)
            part1[core, used, :] = part1[core, used, :] + pair1_in[...]
            rs1_send(pieces[:1])

        def rs1_finish():
            rows_wait(part1.at[0], (PLANE - 1) * rows1, rs1_sem.at[0], rs1_sem.at[1])
            for p in pieces:
                total = rs1_in[p.num, 0, 0:p.rows, :]
                for i in range(1, PLANE):
                    total = total + rs1_in[p.num, i, 0:p.rows, :]
                x_in[p.num, coord[p.cross], pl.ds(0, p.rows), :] = total
            start([rcopy(stage(x_in, p, coord[p.cross]), stage(x_in, p, coord[p.cross]), x_sem.at[0], x_sem.at[1], peer(p.across(step)))
                   for step in (2, 1, 3) for p in pieces])

        def x1_finish():
            rows_wait(part1.at[0], (SIDE - 1) * rows1, x_sem.at[0], x_sem.at[1])
            for p in pieces:
                total = x_in[p.num, 0, 0:p.rows, :]
                for i in range(1, SIDE):
                    total = total + x_in[p.num, i, 0:p.rows, :]
                res1[core, pl.ds(pl.multiple_of(p.base + plane_id(p) * p.rows, 8), p.rows), :] = total
            start([rcopy(chunk1(res1, p, plane_id(p)), chunk1(res1, p, plane_id(p)), ag1_s, ag1_r.at[hops(ab) - 1], peer(p.steps(ab)))
                   for ab in PLANE_PEERS for p in pieces])
            start([back1(p, plane_id(p)) for p in pieces])

        def back1(p, i):
            return rcopy(chunk1(res1, p, i), chunk1(res1, p, i), back1_sem.at[0], back1_sem.at[1], mate)

        def ag1_finish():
            for n in range(1, 5):
                near_n = [ab for ab in PLANE_PEERS if hops(ab) == n]
                rows_wait(part1.at[0], len(near_n) * rows1, None, ag1_r.at[n - 1])
                start([back1(p, plane_id(p, ab)) for ab in near_n for p in pieces])
            rows_wait(part1.at[0], (PLANE - 1) * rows1, ag1_s, None)

        def back1_finish():
            rows_wait(part1.at[0], PLANE * rows1, back1_sem.at[0], back1_sem.at[1])

        my_cube = coord[0] + SIDE * (coord[1] + SIDE * coord[2])
        pair2 = rcopy(part2.at[pl.ds(0, n_slab * slab2), :], pair2_in, pair2_sem.at[0], pair2_sem.at[1], mate)

        def cube_id(steps):
            return moved(0, steps[0]) + SIDE * (moved(1, steps[1]) + SIDE * moved(2, steps[2]))

        def rs2_start():
            pair2.wait_recv()
            used = pl.ds(0, n_slab * slab2)
            part2[used, :] = part2[used, :] + pair2_in[...]
            start([rcopy(rows_of(part2, rows2, cube_id(st)), rs2_in.at[my_cube], rs2_sem.at[0], rs2_sem.at[1], peer(st)) for st in CUBE_PEERS])
            rs2_in[my_cube] = part2[pl.ds(pl.multiple_of(my_cube * rows2, 8), rows2), :]

        def rs2_finish():
            rows_wait(part2, (CUBE - 1) * rows2, rs2_sem.at[0], rs2_sem.at[1])
            sums = [rs2_in[i] for i in range(CUBE)]
            while len(sums) > 1:
                sums = [a + b for a, b in zip(sums[::2], sums[1::2])]
            res2[pl.ds(pl.multiple_of(my_cube * rows2, 8), rows2), :] = sums[0]
            mine = rows_of(res2, rows2, my_cube)
            start([rcopy(mine, mine, ag2_s, ag2_r.at[hops(st) - 1], peer(st)) for st in CUBE_PEERS])
            back2(my_cube).start()

        def back2(i):
            return rcopy(rows_of(res2, rows2, i), rows_of(res2, rows2, i), back2_sem.at[0], back2_sem.at[1], mate)

        def ag2_finish():
            for n in range(1, 7):
                near_n = [st for st in CUBE_PEERS if hops(st) == n]
                rows_wait(part2, len(near_n) * rows2, None, ag2_r.at[n - 1])
                start([back2(cube_id(st)) for st in near_n])
            rows_wait(part2, (CUBE - 1) * rows2, ag2_s, None)
            rows_wait(part2, CUBE * rows2, back2_sem.at[0], None)

        def on(which, name, *steps):
            @pl.when(core == which)
            def _():
                with jax.named_scope(name):
                    for step in steps:
                        step()

        def run(name, *steps):
            with jax.named_scope(name):
                for step in steps:
                    step()

        run("half_mate", lambda: first_half(1 - core))
        run("pair1_start", pair1.start)
        run("half_own", lambda: first_half(core))
        with jax.named_scope("e0"):
            e0[...] = dot(w0[...], ft[...], 1, 0).astype(BF16)
        with jax.named_scope("gossip3"):
            gossip_wait(3)
            gossip_send(4)
        run("pair1_wait", pair1.wait)
        run("rs1_start", rs1_start)
        with jax.named_scope("o0"):
            o0[...] = dot(e0[...], ahalo[...], 1, 0).astype(BF16)

        with jax.named_scope("z_wait"):
            link_wait(sz, haloz, zcp_sem, 0)
            link_wait(sz, haloz, zcp_sem, 1)
        run("rs1_start_x", lambda: rs1_send(pieces[1:]))
        with jax.named_scope("h1h"):
            h1h = jnp.maximum(dot(w0[...], haloz[...], 0, 0), 0.0).astype(BF16)
        with jax.named_scope("z1"):
            z1 = (z1acc[...] + dot(h1h, ahalo[...], 1, 1)).astype(BF16)
        with jax.named_scope("dw2"):
            dw2 = dot(g[...], z1, 1, 1)
            for s in range(n_slab):
                part2[pl.ds(s * slab2, cls), :] = dw2[:, s * 128:(s + 1) * 128]
        on(0, "pair2_start", pair2.start)
        with jax.named_scope("o_start"):
            start(ocp)
            gossip_wait(4)
        with jax.named_scope("gfacc"):
            gfacc[...] = dot(e0[...], aint[...], 1, 0)
        on(1, "rs2_start", rs2_start)
        run("rs1_finish", rs1_finish)
        with jax.named_scope("o_wait"):
            link_wait(o0, r0, ocp_sem, 0)
            link_wait(o0, r0, ocp_sem, 1)
        with jax.named_scope("gf"):
            gf_out[...] = gfacc[...] + dot(r0[...], pt[...], 1, 1)
        run("x1_finish", x1_finish)
        on(1, "rs2_finish", rs2_finish)
        run("ag1_finish", ag1_finish)
        on(1, "ag2_finish", ag2_finish)
        run("back1_finish", back1_finish)
        on(0, "back2_wait", lambda: rows_wait(part2, CUBE * rows2, None, back2_sem.at[1]), pair2.wait_send)
        with jax.named_scope("outs"):
            for s in range(n_slab):
                h, q = s // (n_slab // 2), s % (n_slab // 2)
                dw1_out[:, s * 128:(s + 1) * 128] = res1[h, pl.ds(q * slab1, feat), :]
                dw2_out[:, s * 128:(s + 1) * 128] = res2[pl.ds(s * slab2, cls), :]

    V = pltpu.VMEM
    D = pltpu.SemaphoreType.DMA
    link_sems = [D((2, 2))] * 4
    scratch = [
        V((feat, nodes), BF16), V((nodes, nodes), BF16), V((nodes, all_slots), BF16), V((LINKS, slots), jnp.int32),
        V((feat, hid), BF16), V((cls, hid), BF16), V((cls, nodes), BF16),
        V((nodes, all_slots), BF16), V((hid, nodes), BF16), V((feat, nodes), BF16), V((hid, nodes), BF16), V((feat, nodes), BF16),
        V((feat, all_slots), BF16), V((feat, all_slots), BF16), V((hid, all_slots), BF16), V((hid, all_slots), BF16),
        V((feat, all_slots), BF16), V((feat, all_slots), BF16), V((feat, all_slots), BF16), V((feat, all_slots), BF16),
        V((feat, nodes), F32), V((hid, nodes), F32), V((hid, nodes), F32), V((feat, nodes), F32),
        V((2, end1, 128), F32), V((end2, 128), F32), V((half_rows, 128), F32), V((n_slab * slab2, 128), F32),
        V((3, PLANE, max(share), 128), F32), V((CUBE, rows2, 128), F32), V((3, SIDE, max(share), 128), F32), V((2, end1, 128), F32), V((end2, 128), F32),
        D((7,)), *link_sems, D((2,)), D((2,)), D((2,)), D((2,)), D((2,)), D, D((4,)), D, D((6,)), D((2,)), D((2,)), pltpu.SemaphoreType.REGULAR((5,)),
    ]
    out_bytes = 4 * (slab1 * hid + slab2 * hid + slab1 * nodes)
    any_spec = pl.BlockSpec(memory_space=pl.ANY)
    vmem_spec = pl.BlockSpec(memory_space=pltpu.VMEM)
    return pl.pallas_call(
        kernel,
        out_shape=(pltpu.VMEM((feat, hid), F32), pltpu.VMEM((cls, hid), F32), pltpu.VMEM((feat, nodes), F32)),
        in_specs=[any_spec] * 7,
        out_specs=(vmem_spec, vmem_spec, vmem_spec),
        scratch_shapes=scratch,
        compiler_params=pltpu.CompilerParams(collective_id=0, has_side_effects=True, vmem_limit_bytes=VMEM_BYTES - out_bytes - 65536),
        name="gcn_backward",
    )


def write_out(feat, hid, cls, nodes):
    def kernel(dw1, dw2, gf, dw1_out, dw2_out, gf_out, sems):
        copies = [pltpu.make_async_copy(a, b, sems.at[i]) for i, (a, b) in enumerate(((gf, gf_out), (dw1, dw1_out), (dw2, dw2_out)))]
        for cp in copies:
            cp.start()
        for cp in copies:
            cp.wait()

    return pl.pallas_call(
        kernel,
        out_shape=(jax.ShapeDtypeStruct((feat, hid), F32), jax.ShapeDtypeStruct((cls, hid), F32), jax.ShapeDtypeStruct((feat, nodes), F32)),
        in_specs=[pl.BlockSpec(memory_space=pltpu.VMEM)] * 3,
        out_specs=(pl.BlockSpec(memory_space=pl.ANY),) * 3,
        scratch_shapes=[pltpu.SemaphoreType.DMA((3,))],
        compiler_params=pltpu.CompilerParams(vmem_limit_bytes=4 * 1024 * 1024),
        name="write_out",
    )


def solution(mesh):
    axis_size = mesh.shape["nodes"]
    row_spec = P(("graph", "nodes"), None)
    replicated = P(None, None)
    part_spec = P("graph", None)

    def device_step(node_feats, a_int, a_halo, send_idx, w_first, w_second, grad_out):
        nodes, feat = node_feats.shape
        hid, cls = w_second.shape
        call = build(axis_size, nodes, feat, hid, cls, send_idx.shape[1])
        dw1, dw2, gf = call(node_feats.T, a_int, a_halo, send_idx, w_first, w_second.T, grad_out.T)
        dw1, dw2, gf = write_out(feat, hid, cls, nodes)(dw1, dw2, gf)
        return dw1, dw2.T, gf.T

    return jax.shard_map(device_step, mesh=mesh, in_specs=(row_spec, row_spec, row_spec, row_spec, replicated, replicated, row_spec), out_specs=(part_spec, part_spec, row_spec), check_vma=False)
```

time: 262 us -> 44.3 us (0.17)
  waiting for transfers between devices: 136 us -> 0 us
  starting transfers between devices: 46.3 us -> 0 us
  Pallas kernels: 0 us -> 43.6 us
  local copies, waits for them, and re-layouts: 24.8 us -> 0 us
  matrix products: 20.8 us -> 0 us
  other arithmetic: 19.1 us -> 0 us
  between operations: 14.3 us -> 0.64 us
    psum x1 -> x0, waiting for transfers between devices: 136 us -> none  [device_step(): dw_first = lax.psum(contract_rows(z_first, grad_pre), 'nodes')]
    ppermute x16 -> x0, starting transfers between devices: 46.3 us -> none  [the longest x8 26.5 us: aggregate_back(): lax.ppermute(outward[link * num_slots:(link + 1) * num_slots], 'nodes', s...]
    pallas_call x0 -> x2, Pallas kernels: none -> 43.6 us  [the longest x1 42.3 us: device_step(): call(node_feats.T, a_int, a_halo, send_idx, w_first, w_second.T, grad_out.T)]
    dot_general x12 -> x0, matrix products: 20.8 us -> none  [the longest x6 12.6 us: contract_rows(): lax.dot_general(left_rows, right_rows, (((0,), (0,)), ((), ())), preferre...]
    scatter-add x2 -> x0, other arithmetic: 13.5 us -> none  [aggregate_back(): return inner_sum.at[send_idx.reshape(-1)].add(returned)]
    unnamed x42 -> x0, local copies, waits for them, and re-layouts: 9.77 us -> none
    gather x2 -> x0, local copies, waits for them, and re-layouts: 4.56 us -> none  [halo_rows(): sent_rows = jnp.take(features, send_idx, axis=0)]
    dot_general x2 -> x0, local copies, waits for them, and re-layouts: 4.54 us -> none  [contract_rows(): lax.dot_general(left_rows, right_rows, (((0,), (0,)), ((), ())), preferre...]
  transfers between devices with their start and end apart: 17 -> 0, of which waited for: 1 -> 0; matrix products, arithmetic and copies ran while one was open for 20% -> 0% of each run, Pallas kernels for 0% -> 0%
where the time goes in v3:
time: 44.3 us; the launch traced here: 44.2 us
  Pallas kernels  43.6 us (98%)
  between operations  0.64 us (1%)
    pallas_call x1, Pallas kernels, device_step(): call(node_feats.T, a_int, a_halo, send_idx, w_first, w_second.T, grad_out.T)  42.3 us
    pallas_call x1, Pallas kernels, device_step(): dw1, dw2, gf = write_out(feat, hid, cls, nodes)(dw1, dw2, gf)  1.33 us

profile of v3, /device:TPU:1, one launch (start us, length us, event | category | flops | bytes accessed | tf_op | source)
XLA Modules:
  0.0 44.2 jit_solution(6843417864769573566)
XLA Ops:
  0.6 42.3 %gcn_backward.1 = (f32[300,512]{1,0:T(8,128)S(1)}, f32[100,512]{1,0:T(8,128)S(1)}, f32[300,1024]{1,0:T(8,128)S(1)}) custom-call(bf16[300,1024]{1,0:T(8,128)(2,1)} %bitcast.5, bf16[1024,1024]{1,0:T(8,128)(2,1)} %aint_hbm.1, bf16[1024,512]{1,0:T(8,128)(2,1)} %ahalo_hbm.1, s32[4,128]{1,0:T(4,128)} %idx_hbm.1, bf16[300,512]{1,0:T(8,128)(2,1)} %w0_hbm.1, ...), custom_call_target="tpu_custom_call" | custom-call | tf_op jit(solution)/shard_map/gcn_backward/pallas_call | solution.py:436
  42.9 1.3 %write_out.1 = (f32[300,512]{1,0:T(8,128)}, f32[100,512]{1,0:T(8,128)}, f32[300,1024]{1,0:T(8,128)}) custom-call(f32[300,512]{1,0:T(8,128)S(1)} %get-tuple-element.9.dw1, f32[100,512]{1,0:T(8,128)S(1)} %get-tuple-element.10.dw2, f32[300,1024]{1,0:T(8,128)S(1)} %get-tuple-element.11.gf), custom_call_target="tpu_custom_call" | custom-call | tf_op jit(solution)/shard_map/write_out/pallas_call | solution.py:437

commit v4 on v3

--- a/solution.py
+++ b/solution.py
@@ -13,6 +13,7 @@
 OFFSETS = (1, -1, 2, -2)
 LINKS = 4
 VMEM_BYTES = 67043328
+WRITES = 4
 
 
 def dot(a, b, ca, cb):
@@ -25,6 +26,16 @@
 
 PLANE_PEERS = sorted(((a, b) for a in range(SIDE) for b in range(SIDE) if a or b), key=hops, reverse=True)
 CUBE_PEERS = sorted(((a, b, c) for a in range(SIDE) for b in range(SIDE) for c in range(SIDE) if a or b or c), key=hops, reverse=True)
+
+
+RELEASE = ((0.0, 0.5, 0.9, 1.1), (0.0, 0.6, 1.2, 1.4), (0.0, 0.9, 1.8, 2.4))
+
+
+def release_order(dims):
+    spots = [()]
+    for _ in dims:
+        spots = [s + (c,) for s in spots for c in range(SIDE)]
+    return sorted(spots, key=lambda s: sum(RELEASE[d][c] for d, c in zip(dims, s)))
 
 
 class Piece:
@@ -67,13 +78,19 @@
                z0acc, d1acc, z1acc, gfacc,
                part1, part2, pair1_in, pair2_in, rs1_in, rs2_in, x_in, res1, res2,
                in_sem, fwd_sem, bwd_sem, zcp_sem, ocp_sem,
-               pair1_sem, pair2_sem, rs1_sem, rs2_sem, x_sem, ag1_s, ag1_r, ag2_s, ag2_r, back1_sem, back2_sem, gossip):
+               pair1_sem, pair2_sem, rs1_sem, rs2_sem, x_r, ag1_r, ag2_r, back1_s, back2_s, early_s, gossip):
         me = lax.axis_index("nodes")
         core = lax.rem(me, 2)
         coord = (lax.rem(me // 2, SIDE), lax.rem(me // (2 * SIDE), SIDE), me // (2 * SIDE * SIDE))
         stride = (2, 2 * SIDE, 2 * SIDE * SIDE)
         mate = me + 1 - 2 * core
 
+        def ring_steps(dim, c):
+            d = lax.rem(coord[dim] + (SIDE - c), SIDE)
+            return d * (SIDE - d) - d * (SIDE - d) // 3 * 2
+
+        away = [[ring_steps(dim, c) for c in range(SIDE)] for dim in range(3)]
+
         def moved(dim, step):
             return lax.rem(coord[dim] + step, SIDE)
 
@@ -97,11 +114,15 @@
             return ref.at[:, pl.ds(k * slots, slots)]
 
         def link_copies(src, dst, sems, sign):
-            return [rcopy(lanes(src, k), lanes(dst, k), sems.at[0, k // 2], sems.at[1, k // 2], near(sign * OFFSETS[k])) for k in range(LINKS)]
+            return [rcopy(lanes(src, k), lanes(dst, k), sems.at[0], sems.at[1 + k // 2], near(sign * OFFSETS[k])) for k in range(LINKS)]
 
         def link_wait(src, dst, sems, i):
             both = pl.ds(2 * i * slots, 2 * slots)
-            rcopy(src.at[:, both], dst.at[:, both], sems.at[0, i], sems.at[1, i], mate).wait()
+            rcopy(src.at[:, both], dst.at[:, both], sems.at[0], sems.at[1 + i], mate).wait_recv()
+
+        def links_sent():
+            for src, dst, sems in ((s0, halo0, fwd_sem), (o1, r1, bwd_sem), (sz, haloz, zcp_sem), (o0, r0, ocp_sem)):
+                rcopy(src, dst, sems.at[0], sems.at[1], mate).wait_send()
 
         def start(copies):
             for cp in copies:
@@ -111,22 +132,30 @@
             for cp in copies:
                 cp.wait()
 
-        loads = [pltpu.make_async_copy(a, b, in_sem.at[i]) for i, (a, b) in enumerate((
-            (idx_hbm, idx), (h0_hbm, h0), (g_hbm, g), (w1_hbm, w1), (ahalo_hbm, ahalo), (aint_hbm, aint), (w0_hbm, w0)))]
-        start(loads)
-        ld_idx, ld_h0, ld_g, ld_w1, ld_ahalo, ld_aint, ld_w0 = loads
+        def on(which, name, *steps):
+            @pl.when(core == which)
+            def _():
+                with jax.named_scope(name):
+                    for step in steps:
+                        step()
+
         barrier = pltpu.get_barrier_semaphore()
         ring = [peer(tuple(step if d == dim else 0 for d in range(3))) for dim in range(3) for step in (1, SIDE - 1)]
         greeted = [near(o) for o in OFFSETS] + [mate] + ring
         for d in greeted:
             signal(barrier, d)
 
+        loads = [pltpu.make_async_copy(a, b, in_sem.at[i]) for i, (a, b) in enumerate((
+            (idx_hbm, idx), (h0_hbm, h0), (g_hbm, g), (w1_hbm, w1), (ahalo_hbm, ahalo), (aint_hbm, aint), (w0_hbm, w0)))]
+        start(loads)
+        ld_idx, ld_h0, ld_g, ld_w1, ld_ahalo, ld_aint, ld_w0 = loads
+
         def gossip_send(i):
             for d in ring:
-                signal(gossip.at[i], d)
+                signal(gossip.at[i % 2], d)
 
         def gossip_wait(i):
-            pl.semaphore_wait(gossip.at[i], len(ring))
+            pl.semaphore_wait(gossip.at[i % 2], len(ring))
 
         part1[...] = jnp.zeros_like(part1)
         part2[...] = jnp.zeros_like(part2)
@@ -150,15 +179,13 @@
             ld_h0.wait()
         with jax.named_scope("s0"):
             s0[:, upper] = dot(h0[...], pt[:, upper], 1, 0).astype(BF16)
+        with jax.named_scope("s0_low"):
+            select_rows((0, 1))
+            s0[:, lower] = dot(h0[...], pt[:, lower], 1, 0).astype(BF16)
         with jax.named_scope("barrier"):
             pl.semaphore_wait(barrier, len(greeted))
         with jax.named_scope("fwd_start"):
-            start(fwd[2:])
-        with jax.named_scope("s0_low"):
-            select_rows((0, 1))
-            s0[:, lower] = dot(h0[...], pt[:, lower], 1, 0).astype(BF16)
-        with jax.named_scope("fwd_start_low"):
-            start(fwd[:2])
+            start(fwd[2:] + fwd[:2])
             gossip_send(0)
         with jax.named_scope("e1"):
             ld_g.wait()
@@ -167,26 +194,34 @@
         with jax.named_scope("o1"):
             ld_ahalo.wait()
             o1[...] = dot(e1[...], ahalo[...], 1, 0).astype(BF16)
-        with jax.named_scope("bwd_start"):
-            start(bwd[2:] + bwd[:2])
+        on(0, "bwd_start0", lambda: start([bwd[2], bwd[0], bwd[1]]))
+        on(1, "bwd_start1", lambda: start([bwd[3], bwd[1], bwd[0]]))
         with jax.named_scope("z0acc"):
             ld_aint.wait()
             z0acc[...] = dot(h0[...], aint[...], 1, 1)
+        on(0, "bwd_rest0", bwd[3].start)
+        on(1, "bwd_rest1", bwd[2].start)
         with jax.named_scope("gossip0"):
             gossip_wait(0)
             gossip_send(1)
         with jax.named_scope("d1acc"):
             d1acc[...] = dot(e1[...], aint[...], 1, 0)
 
-        with jax.named_scope("fwd_wait"):
+        with jax.named_scope("fwd_wait_up"):
+            link_wait(s0, halo0, fwd_sem, 1)
+        with jax.named_scope("z0_up"):
+            z0acc[...] = z0acc[...] + dot(halo0[:, upper], ahalo[:, upper], 1, 1)
+        with jax.named_scope("fwd_wait_low"):
             link_wait(s0, halo0, fwd_sem, 0)
-            link_wait(s0, halo0, fwd_sem, 1)
         with jax.named_scope("z0"):
-            z0[...] = (z0acc[...] + dot(halo0[...], ahalo[...], 1, 1)).astype(BF16)
-        with jax.named_scope("sz"):
-            sz[...] = dot(z0[...], pt[...], 1, 0).astype(BF16)
-        with jax.named_scope("z_start"):
-            start(zcp[2:] + zcp[:2])
+            z0[...] = (z0acc[...] + dot(halo0[:, lower], ahalo[:, lower], 1, 1)).astype(BF16)
+        halves = (zcp[:2], zcp[2:])
+        for n in range(2):
+            with jax.named_scope("sz%d" % n):
+                cols = pl.ds(pl.multiple_of((core if n else 1 - core) * 2 * slots, 2 * slots), 2 * slots)
+                sz[:, cols] = dot(z0[...], pt[:, cols], 1, 0).astype(BF16)
+            on(0, "z_start%d" % n, lambda: start(halves[1 - n]))
+            on(1, "z_start%d" % n, lambda: start(halves[n]))
         with jax.named_scope("gossip1"):
             gossip_wait(1)
             gossip_send(2)
@@ -244,7 +279,7 @@
         def rs1_start():
             used = pl.ds(0, half_rows)
             part1[core, used, :] = part1[core, used, :] + pair1_in[...]
-            rs1_send(pieces[:1])
+            rs1_send(pieces)
 
         def rs1_finish():
             rows_wait(part1.at[0], (PLANE - 1) * rows1, rs1_sem.at[0], rs1_sem.at[1])
@@ -253,32 +288,38 @@
                 for i in range(1, PLANE):
                     total = total + rs1_in[p.num, i, 0:p.rows, :]
                 x_in[p.num, coord[p.cross], pl.ds(0, p.rows), :] = total
-            start([rcopy(stage(x_in, p, coord[p.cross]), stage(x_in, p, coord[p.cross]), x_sem.at[0], x_sem.at[1], peer(p.across(step)))
+            start([rcopy(stage(x_in, p, coord[p.cross]), stage(x_in, p, coord[p.cross]), rs1_sem.at[0], x_r, peer(p.across(step)))
                    for step in (2, 1, 3) for p in pieces])
 
         def x1_finish():
-            rows_wait(part1.at[0], (SIDE - 1) * rows1, x_sem.at[0], x_sem.at[1])
+            rows_wait(part1.at[0], (SIDE - 1) * rows1, rs1_sem.at[0], x_r)
             for p in pieces:
                 total = x_in[p.num, 0, 0:p.rows, :]
                 for i in range(1, SIDE):
                     total = total + x_in[p.num, i, 0:p.rows, :]
                 res1[core, pl.ds(pl.multiple_of(p.base + plane_id(p) * p.rows, 8), p.rows), :] = total
-            start([rcopy(chunk1(res1, p, plane_id(p)), chunk1(res1, p, plane_id(p)), ag1_s, ag1_r.at[hops(ab) - 1], peer(p.steps(ab)))
-                   for ab in PLANE_PEERS for p in pieces])
-            start([back1(p, plane_id(p)) for p in pieces])
+            mine = [chunk1(res1, p, plane_id(p)) for p in pieces]
+            order = [release_order(p.plane) for p in pieces]
+            for spots in zip(*order):
+                for p, ref, (a, b) in zip(pieces, mine, spots):
+                    steps = away[p.plane[0]][a] + away[p.plane[1]][b]
+                    d = core + a * stride[p.plane[0]] + b * stride[p.plane[1]] + coord[p.cross] * stride[p.cross]
+                    rcopy(ref, ref, rs1_sem.at[0], ag1_r.at[steps], d + jnp.where(steps == 0, mate - me, 0)).start()
 
         def back1(p, i):
-            return rcopy(chunk1(res1, p, i), chunk1(res1, p, i), back1_sem.at[0], back1_sem.at[1], mate)
-
-        def ag1_finish():
-            for n in range(1, 5):
-                near_n = [ab for ab in PLANE_PEERS if hops(ab) == n]
-                rows_wait(part1.at[0], len(near_n) * rows1, None, ag1_r.at[n - 1])
-                start([back1(p, plane_id(p, ab)) for ab in near_n for p in pieces])
-            rows_wait(part1.at[0], (PLANE - 1) * rows1, ag1_s, None)
+            return rcopy(chunk1(res1, p, i), chunk1(res1, p, i), back1_s, ag1_r.at[0], mate)
+
+        def ag1_step(n):
+            near_n = [ab for ab in PLANE_PEERS if hops(ab) == n]
+            rows_wait(part1.at[0], len(near_n) * rows1, None, ag1_r.at[n])
+            start([back1(p, plane_id(p, ab)) for ab in near_n for p in pieces])
 
         def back1_finish():
-            rows_wait(part1.at[0], PLANE * rows1, back1_sem.at[0], back1_sem.at[1])
+            rows_wait(part1.at[0], PLANE * rows1, None, ag1_r.at[0])
+
+        def back1_sent():
+            rows_wait(part1.at[0], PLANE * rows1, rs1_sem.at[0], None)
+            rows_wait(part1.at[0], (PLANE - 1) * rows1, back1_s, None)
 
         my_cube = coord[0] + SIDE * (coord[1] + SIDE * coord[2])
         pair2 = rcopy(part2.at[pl.ds(0, n_slab * slab2), :], pair2_in, pair2_sem.at[0], pair2_sem.at[1], mate)
@@ -300,26 +341,28 @@
                 sums = [a + b for a, b in zip(sums[::2], sums[1::2])]
             res2[pl.ds(pl.multiple_of(my_cube * rows2, 8), rows2), :] = sums[0]
             mine = rows_of(res2, rows2, my_cube)
-            start([rcopy(mine, mine, ag2_s, ag2_r.at[hops(st) - 1], peer(st)) for st in CUBE_PEERS])
-            back2(my_cube).start()
+            for a, b, c in release_order((0, 1, 2)):
+                steps = away[0][a] + away[1][b] + away[2][c]
+                d = core + a * stride[0] + b * stride[1] + c * stride[2]
+                rcopy(mine, mine, rs2_sem.at[0], ag2_r.at[steps], d + jnp.where(steps == 0, mate - me, 0)).start()
+                if (a, b, c) == (0, 0, 0):
+                    pl.when(me != 1)(rcopy(mine, mine, early_s, ag2_r.at[0], 0).start)
 
         def back2(i):
-            return rcopy(rows_of(res2, rows2, i), rows_of(res2, rows2, i), back2_sem.at[0], back2_sem.at[1], mate)
+            return rcopy(rows_of(res2, rows2, i), rows_of(res2, rows2, i), back2_s, ag2_r.at[0], mate)
+
+        def ag2_step(n):
+            near_n = [st for st in CUBE_PEERS if hops(st) == n]
+            rows_wait(part2, len(near_n) * rows2, None, ag2_r.at[n])
+            pl.when(me != 1)(lambda: start([back2(cube_id(st)) for st in near_n]))
 
         def ag2_finish():
-            for n in range(1, 7):
-                near_n = [st for st in CUBE_PEERS if hops(st) == n]
-                rows_wait(part2, len(near_n) * rows2, None, ag2_r.at[n - 1])
-                start([back2(cube_id(st)) for st in near_n])
-            rows_wait(part2, (CUBE - 1) * rows2, ag2_s, None)
-            rows_wait(part2, CUBE * rows2, back2_sem.at[0], None)
-
-        def on(which, name, *steps):
-            @pl.when(core == which)
+            rows_wait(part2, CUBE * rows2, rs2_sem.at[0], None)
+
+            @pl.when(me != 1)
             def _():
-                with jax.named_scope(name):
-                    for step in steps:
-                        step()
+                rows_wait(part2, (CUBE - 1) * rows2, back2_s, None)
+                rows_wait(part2, rows2, early_s, None)
 
         def run(name, *steps):
             with jax.named_scope(name):
@@ -336,49 +379,58 @@
             gossip_send(4)
         run("pair1_wait", pair1.wait)
         run("rs1_start", rs1_start)
-        with jax.named_scope("o0"):
-            o0[...] = dot(e0[...], ahalo[...], 1, 0).astype(BF16)
-
-        with jax.named_scope("z_wait"):
-            link_wait(sz, haloz, zcp_sem, 0)
-            link_wait(sz, haloz, zcp_sem, 1)
-        run("rs1_start_x", lambda: rs1_send(pieces[1:]))
-        with jax.named_scope("h1h"):
-            h1h = jnp.maximum(dot(w0[...], haloz[...], 0, 0), 0.0).astype(BF16)
-        with jax.named_scope("z1"):
-            z1 = (z1acc[...] + dot(h1h, ahalo[...], 1, 1)).astype(BF16)
+
+        def z1_half(n):
+            cols = pl.ds(pl.multiple_of((core if n else 1 - core) * 2 * slots, 2 * slots), 2 * slots)
+            on(0, "z_wait%d" % n, lambda: link_wait(sz, haloz, zcp_sem, 1 - n))
+            on(1, "z_wait%d" % n, lambda: link_wait(sz, haloz, zcp_sem, n))
+            with jax.named_scope("z1_%d" % n):
+                h1h = jnp.maximum(dot(w0[...], haloz[:, cols], 0, 0), 0.0).astype(BF16)
+                return z1acc[...] + dot(h1h, ahalo[:, cols], 1, 1)
+
+        z1acc[...] = z1_half(0)
+        z1 = z1_half(1).astype(BF16)
         with jax.named_scope("dw2"):
             dw2 = dot(g[...], z1, 1, 1)
             for s in range(n_slab):
                 part2[pl.ds(s * slab2, cls), :] = dw2[:, s * 128:(s + 1) * 128]
         on(0, "pair2_start", pair2.start)
-        with jax.named_scope("o_start"):
-            start(ocp)
+        with jax.named_scope("gossip4"):
             gossip_wait(4)
+        with jax.named_scope("o0"):
+            o0[...] = dot(e0[...], ahalo[...], 1, 0).astype(BF16)
         with jax.named_scope("gfacc"):
             gfacc[...] = dot(e0[...], aint[...], 1, 0)
         on(1, "rs2_start", rs2_start)
         run("rs1_finish", rs1_finish)
+        with jax.named_scope("o_start"):
+            start(ocp)
+        run("x1_finish", x1_finish)
+        on(1, "rs2_finish", rs2_finish)
         with jax.named_scope("o_wait"):
             link_wait(o0, r0, ocp_sem, 0)
             link_wait(o0, r0, ocp_sem, 1)
         with jax.named_scope("gf"):
             gf_out[...] = gfacc[...] + dot(r0[...], pt[...], 1, 1)
-        run("x1_finish", x1_finish)
-        on(1, "rs2_finish", rs2_finish)
-        run("ag1_finish", ag1_finish)
-        on(1, "ag2_finish", ag2_finish)
+        for n in range(1, 7):
+            if n <= 4:
+                run("ag1_%d" % n, lambda: ag1_step(n))
+            on(1, "ag2_%d" % n, lambda: ag2_step(n))
         run("back1_finish", back1_finish)
-        on(0, "back2_wait", lambda: rows_wait(part2, CUBE * rows2, None, back2_sem.at[1]), pair2.wait_send)
+        on(0, "back2_wait", lambda: rows_wait(part2, CUBE * rows2, None, ag2_r.at[0]), pair2.wait_send)
         with jax.named_scope("outs"):
             for s in range(n_slab):
                 h, q = s // (n_slab // 2), s % (n_slab // 2)
                 dw1_out[:, s * 128:(s + 1) * 128] = res1[h, pl.ds(q * slab1, feat), :]
                 dw2_out[:, s * 128:(s + 1) * 128] = res2[pl.ds(s * slab2, cls), :]
 
+        run("links_sent", links_sent)
+        run("back1_sent", back1_sent)
+        on(1, "ag2_finish", ag2_finish)
+
     V = pltpu.VMEM
     D = pltpu.SemaphoreType.DMA
-    link_sems = [D((2, 2))] * 4
+    link_sems = [D((3,))] * 4
     scratch = [
         V((feat, nodes), BF16), V((nodes, nodes), BF16), V((nodes, all_slots), BF16), V((LINKS, slots), jnp.int32),
         V((feat, hid), BF16), V((cls, hid), BF16), V((cls, nodes), BF16),
@@ -388,7 +440,7 @@
         V((feat, nodes), F32), V((hid, nodes), F32), V((hid, nodes), F32), V((feat, nodes), F32),
         V((2, end1, 128), F32), V((end2, 128), F32), V((half_rows, 128), F32), V((n_slab * slab2, 128), F32),
         V((3, PLANE, max(share), 128), F32), V((CUBE, rows2, 128), F32), V((3, SIDE, max(share), 128), F32), V((2, end1, 128), F32), V((end2, 128), F32),
-        D((7,)), *link_sems, D((2,)), D((2,)), D((2,)), D((2,)), D((2,)), D, D((4,)), D, D((6,)), D((2,)), D((2,)), pltpu.SemaphoreType.REGULAR((5,)),
+        D((7,)), *link_sems, D((2,)), D((2,)), D((2,)), D((2,)), D, D((5,)), D((7,)), D, D, D, pltpu.SemaphoreType.REGULAR((2,)),
     ]
     out_bytes = 4 * (slab1 * hid + slab2 * hid + slab1 * nodes)
     any_spec = pl.BlockSpec(memory_space=pl.ANY)
@@ -406,7 +458,11 @@
 
 def write_out(feat, hid, cls, nodes):
     def kernel(dw1, dw2, gf, dw1_out, dw2_out, gf_out, sems):
-        copies = [pltpu.make_async_copy(a, b, sems.at[i]) for i, (a, b) in enumerate(((gf, gf_out), (dw1, dw1_out), (dw2, dw2_out)))]
+        pairs = [(dw1, dw1_out), (dw2, dw2_out)]
+        for i in range(WRITES):
+            cols = pl.ds(i * (nodes // WRITES), nodes // WRITES)
+            pairs.append((gf.at[:, cols], gf_out.at[:, cols]))
+        copies = [pltpu.make_async_copy(a, b, sems.at[i]) for i, (a, b) in enumerate(pairs)]
         for cp in copies:
             cp.start()
         for cp in copies:
@@ -417,7 +473,7 @@
         out_shape=(jax.ShapeDtypeStruct((feat, hid), F32), jax.ShapeDtypeStruct((cls, hid), F32), jax.ShapeDtypeStruct((feat, nodes), F32)),
         in_specs=[pl.BlockSpec(memory_space=pltpu.VMEM)] * 3,
         out_specs=(pl.BlockSpec(memory_space=pl.ANY),) * 3,
-        scratch_shapes=[pltpu.SemaphoreType.DMA((3,))],
+        scratch_shapes=[pltpu.SemaphoreType.DMA((2 + WRITES,))],
         compiler_params=pltpu.CompilerParams(vmem_limit_bytes=4 * 1024 * 1024),
         name="write_out",
     )

time: 44.3 us -> 42.8 us (0.966)
  Pallas kernels: 43.6 us -> 42 us
    pallas_call x1, Pallas kernels: 42.3 us -> 40.7 us  [device_step(): call(node_feats.T, a_int, a_halo, send_idx, w_first, w_second.T, grad_out.T)]
where the time goes in v4:
time: 42.8 us; the launch traced here: 42.7 us
  Pallas kernels  42 us (98%)
  between operations  0.64 us (1%)
    pallas_call x1, Pallas kernels, device_step(): call(node_feats.T, a_int, a_halo, send_idx, w_first, w_second.T, grad_out.T)  40.7 us
    pallas_call x1, Pallas kernels, device_step(): dw1, dw2, gf = write_out(feat, hid, cls, nodes)(dw1, dw2, gf)  1.36 us

profile of v4, /device:TPU:1, one launch (start us, length us, event | category | flops | bytes accessed | tf_op | source)
XLA Modules:
  0.0 42.7 jit_solution(12525248855282553914)
XLA Ops:
  0.6 40.7 %gcn_backward.1 = (f32[300,512]{1,0:T(8,128)S(1)}, f32[100,512]{1,0:T(8,128)S(1)}, f32[300,1024]{1,0:T(8,128)S(1)}) custom-call(bf16[300,1024]{1,0:T(8,128)(2,1)} %bitcast.5, bf16[1024,1024]{1,0:T(8,128)(2,1)} %aint_hbm.1, bf16[1024,512]{1,0:T(8,128)(2,1)} %ahalo_hbm.1, s32[4,128]{1,0:T(4,128)} %idx_hbm.1, bf16[300,512]{1,0:T(8,128)(2,1)} %w0_hbm.1, ...), custom_call_target="tpu_custom_call" | custom-call | tf_op jit(solution)/shard_map/gcn_backward/pallas_call | solution.py:492
  41.3 1.4 %write_out.1 = (f32[300,512]{1,0:T(8,128)}, f32[100,512]{1,0:T(8,128)}, f32[300,1024]{1,0:T(8,128)}) custom-call(f32[300,512]{1,0:T(8,128)S(1)} %get-tuple-element.9.dw1, f32[100,512]{1,0:T(8,128)S(1)} %get-tuple-element.10.dw2, f32[300,1024]{1,0:T(8,128)S(1)} %get-tuple-element.11.gf), custom_call_target="tpu_custom_call" | custom-call | tf_op jit(solution)/shard_map/write_out/pallas_call | solution.py:493

commit v5 on v4

--- a/solution.py
+++ b/solution.py
@@ -78,7 +78,7 @@
                z0acc, d1acc, z1acc, gfacc,
                part1, part2, pair1_in, pair2_in, rs1_in, rs2_in, x_in, res1, res2,
                in_sem, fwd_sem, bwd_sem, zcp_sem, ocp_sem,
-               pair1_sem, pair2_sem, rs1_sem, rs2_sem, x_r, ag1_r, ag2_r, back1_s, back2_s, early_s, gossip):
+               pair1_sem, pair2_sem, rs1_sem, rs1_r, rs2_sem, x_s, x_r, ag1_r, ag2_r, back1_s, back2_s, early_s, gossip):
         me = lax.axis_index("nodes")
         core = lax.rem(me, 2)
         coord = (lax.rem(me // 2, SIDE), lax.rem(me // (2 * SIDE), SIDE), me // (2 * SIDE * SIDE))
@@ -271,7 +271,7 @@
             return ref.at[p.num, i, pl.ds(0, p.rows), :]
 
         def rs1_send(group):
-            start([rcopy(chunk1(part1, p, plane_id(p, ab)), stage(rs1_in, p, plane_id(p)), rs1_sem.at[0], rs1_sem.at[1], peer(p.steps(ab)))
+            start([rcopy(chunk1(part1, p, plane_id(p, ab)), stage(rs1_in, p, plane_id(p)), rs1_sem.at[0], rs1_r.at[p.num], peer(p.steps(ab)))
                    for ab in PLANE_PEERS for p in group])
             for p in group:
                 rs1_in[p.num, plane_id(p), pl.ds(0, p.rows), :] = part1[core, pl.ds(pl.multiple_of(p.base + plane_id(p) * p.rows, 8), p.rows), :]
@@ -282,29 +282,29 @@
             rs1_send(pieces)
 
         def rs1_finish():
-            rows_wait(part1.at[0], (PLANE - 1) * rows1, rs1_sem.at[0], rs1_sem.at[1])
             for p in pieces:
+                rows_wait(part1.at[0], (PLANE - 1) * p.rows, None, rs1_r.at[p.num])
                 total = rs1_in[p.num, 0, 0:p.rows, :]
                 for i in range(1, PLANE):
                     total = total + rs1_in[p.num, i, 0:p.rows, :]
+                mine = stage(x_in, p, coord[p.cross])
                 x_in[p.num, coord[p.cross], pl.ds(0, p.rows), :] = total
-            start([rcopy(stage(x_in, p, coord[p.cross]), stage(x_in, p, coord[p.cross]), rs1_sem.at[0], x_r, peer(p.across(step)))
-                   for step in (2, 1, 3) for p in pieces])
+                start([rcopy(mine, mine, x_s, x_r.at[p.num], peer(p.across(step))) for step in (2, 1, 3)])
+            rows_wait(part1.at[0], (PLANE - 1) * rows1, rs1_sem.at[0], None)
 
         def x1_finish():
-            rows_wait(part1.at[0], (SIDE - 1) * rows1, rs1_sem.at[0], x_r)
             for p in pieces:
+                rows_wait(part1.at[0], (SIDE - 1) * p.rows, None, x_r.at[p.num])
                 total = x_in[p.num, 0, 0:p.rows, :]
                 for i in range(1, SIDE):
                     total = total + x_in[p.num, i, 0:p.rows, :]
                 res1[core, pl.ds(pl.multiple_of(p.base + plane_id(p) * p.rows, 8), p.rows), :] = total
-            mine = [chunk1(res1, p, plane_id(p)) for p in pieces]
-            order = [release_order(p.plane) for p in pieces]
-            for spots in zip(*order):
-                for p, ref, (a, b) in zip(pieces, mine, spots):
+                mine = chunk1(res1, p, plane_id(p))
+                for a, b in release_order(p.plane):
                     steps = away[p.plane[0]][a] + away[p.plane[1]][b]
                     d = core + a * stride[p.plane[0]] + b * stride[p.plane[1]] + coord[p.cross] * stride[p.cross]
-                    rcopy(ref, ref, rs1_sem.at[0], ag1_r.at[steps], d + jnp.where(steps == 0, mate - me, 0)).start()
+                    rcopy(mine, mine, rs1_sem.at[0], ag1_r.at[steps], d + jnp.where(steps == 0, mate - me, 0)).start()
+            rows_wait(part1.at[0], (SIDE - 1) * rows1, x_s, None)
 
         def back1(p, i):
             return rcopy(chunk1(res1, p, i), chunk1(res1, p, i), back1_s, ag1_r.at[0], mate)
@@ -399,12 +399,14 @@
             gossip_wait(4)
         with jax.named_scope("o0"):
             o0[...] = dot(e0[...], ahalo[...], 1, 0).astype(BF16)
+            pl.when(me == n_dev - 1)(ocp[3].start)
         with jax.named_scope("gfacc"):
             gfacc[...] = dot(e0[...], aint[...], 1, 0)
         on(1, "rs2_start", rs2_start)
         run("rs1_finish", rs1_finish)
         with jax.named_scope("o_start"):
-            start(ocp)
+            start(ocp[:3])
+            pl.when(me < n_dev - 1)(ocp[3].start)
         run("x1_finish", x1_finish)
         on(1, "rs2_finish", rs2_finish)
         with jax.named_scope("o_wait"):
@@ -440,7 +442,7 @@
         V((feat, nodes), F32), V((hid, nodes), F32), V((hid, nodes), F32), V((feat, nodes), F32),
         V((2, end1, 128), F32), V((end2, 128), F32), V((half_rows, 128), F32), V((n_slab * slab2, 128), F32),
         V((3, PLANE, max(share), 128), F32), V((CUBE, rows2, 128), F32), V((3, SIDE, max(share), 128), F32), V((2, end1, 128), F32), V((end2, 128), F32),
-        D((7,)), *link_sems, D((2,)), D((2,)), D((2,)), D((2,)), D, D((5,)), D((7,)), D, D, D, pltpu.SemaphoreType.REGULAR((2,)),
+        D((7,)), *link_sems, D((2,)), D((2,)), D((1,)), D((3,)), D((2,)), D, D((3,)), D((5,)), D((7,)), D, D, D, pltpu.SemaphoreType.REGULAR((2,)),
     ]
     out_bytes = 4 * (slab1 * hid + slab2 * hid + slab1 * nodes)
     any_spec = pl.BlockSpec(memory_space=pl.ANY)

time: 42.8 us -> 42.4 us (level)
  no operation moved by 1% of the time
where the time goes in v5:
time: 42.4 us; the launch traced here: 42.3 us
  Pallas kernels  41.7 us (98%)
  between operations  0.64 us (2%)
    pallas_call x1, Pallas kernels, device_step(): call(node_feats.T, a_int, a_halo, send_idx, w_first, w_second.T, grad_out.T)  40.3 us
    pallas_call x1, Pallas kernels, device_step(): dw1, dw2, gf = write_out(feat, hid, cls, nodes)(dw1, dw2, gf)  1.36 us

profile of v5, /device:TPU:1, one launch (start us, length us, event | category | flops | bytes accessed | tf_op | source)
XLA Modules:
  0.0 42.3 jit_solution(15435315750607396431)
XLA Ops:
  0.6 40.3 %gcn_backward.1 = (f32[300,512]{1,0:T(8,128)S(1)}, f32[100,512]{1,0:T(8,128)S(1)}, f32[300,1024]{1,0:T(8,128)S(1)}) custom-call(bf16[300,1024]{1,0:T(8,128)(2,1)} %bitcast.5, bf16[1024,1024]{1,0:T(8,128)(2,1)} %aint_hbm.1, bf16[1024,512]{1,0:T(8,128)(2,1)} %ahalo_hbm.1, s32[4,128]{1,0:T(4,128)} %idx_hbm.1, bf16[300,512]{1,0:T(8,128)(2,1)} %w0_hbm.1, ...), custom_call_target="tpu_custom_call" | custom-call | tf_op jit(solution)/shard_map/gcn_backward/pallas_call | solution.py:494
  41.0 1.4 %write_out.1 = (f32[300,512]{1,0:T(8,128)}, f32[100,512]{1,0:T(8,128)}, f32[300,1024]{1,0:T(8,128)}) custom-call(f32[300,512]{1,0:T(8,128)S(1)} %get-tuple-element.9.dw1, f32[100,512]{1,0:T(8,128)S(1)} %get-tuple-element.10.dw2, f32[300,1024]{1,0:T(8,128)S(1)} %get-tuple-element.11.gf), custom_call_target="tpu_custom_call" | custom-call | tf_op jit(solution)/shard_map/write_out/pallas_call | solution.py:495

commit v6 on v5

--- a/solution.py
+++ b/solution.py
@@ -13,7 +13,7 @@
 OFFSETS = (1, -1, 2, -2)
 LINKS = 4
 VMEM_BYTES = 67043328
-WRITES = 4
+WRITES = 1
 
 
 def dot(a, b, ca, cb):
@@ -414,9 +414,9 @@
             link_wait(o0, r0, ocp_sem, 1)
         with jax.named_scope("gf"):
             gf_out[...] = gfacc[...] + dot(r0[...], pt[...], 1, 1)
+        for n in range(1, 5):
+            run("ag1_%d" % n, lambda: ag1_step(n))
         for n in range(1, 7):
-            if n <= 4:
-                run("ag1_%d" % n, lambda: ag1_step(n))
             on(1, "ag2_%d" % n, lambda: ag2_step(n))
         run("back1_finish", back1_finish)
         on(0, "back2_wait", lambda: rows_wait(part2, CUBE * rows2, None, ag2_r.at[0]), pair2.wait_send)

time: 42.4 us -> 42.2 us (level)
  no operation moved by 1% of the time
where the time goes in v6:
time: 42.2 us; the launch traced here: 42.1 us
  Pallas kernels  41.5 us (98%)
  between operations  0.64 us (2%)
    pallas_call x1, Pallas kernels, device_step(): call(node_feats.T, a_int, a_halo, send_idx, w_first, w_second.T, grad_out.T)  40.1 us
    pallas_call x1, Pallas kernels, device_step(): dw1, dw2, gf = write_out(feat, hid, cls, nodes)(dw1, dw2, gf)  1.34 us

profile of v6, /device:TPU:1, one launch (start us, length us, event | category | flops | bytes accessed | tf_op | source)
XLA Modules:
  0.0 42.1 jit_solution(6500234836339505599)
XLA Ops:
  0.6 40.1 %gcn_backward.1 = (f32[300,512]{1,0:T(8,128)S(1)}, f32[100,512]{1,0:T(8,128)S(1)}, f32[300,1024]{1,0:T(8,128)S(1)}) custom-call(bf16[300,1024]{1,0:T(8,128)(2,1)} %bitcast.5, bf16[1024,1024]{1,0:T(8,128)(2,1)} %aint_hbm.1, bf16[1024,512]{1,0:T(8,128)(2,1)} %ahalo_hbm.1, s32[4,128]{1,0:T(4,128)} %idx_hbm.1, bf16[300,512]{1,0:T(8,128)(2,1)} %w0_hbm.1, ...), custom_call_target="tpu_custom_call" | custom-call | tf_op jit(solution)/shard_map/gcn_backward/pallas_call | solution.py:494
  40.8 1.3 %write_out.1 = (f32[300,512]{1,0:T(8,128)}, f32[100,512]{1,0:T(8,128)}, f32[300,1024]{1,0:T(8,128)}) custom-call(f32[300,512]{1,0:T(8,128)S(1)} %get-tuple-element.9.dw1, f32[100,512]{1,0:T(8,128)S(1)} %get-tuple-element.10.dw2, f32[300,1024]{1,0:T(8,128)S(1)} %get-tuple-element.11.gf), custom_call_target="tpu_custom_call" | custom-call | tf_op jit(solution)/shard_map/write_out/pallas_call | solution.py:495
